TPU v7x, 8 devices: a whole 2x2x1 slice. The times are simulated.
8 devices in a mesh: fsdp: 2 (over z, y), ep: 4 (over x, core).
Axes of the slice: x: 2, y: 2, z: 1, core: 2. Of those that a mesh axis runs over, the one named last changes fastest.
Arguments:
- x_tok: bfloat16 [32768, 896], P(('fsdp', 'ep'))
- dy_tok: bfloat16 [32768, 896], P(('fsdp', 'ep'))
- expert_idx: int32 [32768, 8], P(('fsdp', 'ep'))
- gate_val: float32 [32768, 8], P(('fsdp', 'ep'))
- w_one: bfloat16 [256, 896, 256], P('ep', 'fsdp')
- w_two: bfloat16 [256, 256, 896], P('ep', None, 'fsdp')
- w_three: bfloat16 [256, 896, 256], P('ep', 'fsdp')
- ws_one: bfloat16 [896, 256], P('fsdp')
- ws_two: bfloat16 [256, 896], P(None, 'fsdp')
- ws_three: bfloat16 [896, 256], P('fsdp')
Outputs:
- output 1: bfloat16 [32768, 896], P(('fsdp', 'ep'))
- output 2: float32 [32768, 8], P(('fsdp', 'ep'))
- output 3: float32 [256, 896, 256], P('ep', 'fsdp')
- output 4: float32 [256, 256, 896], P('ep', None, 'fsdp')
- output 5: float32 [256, 896, 256], P('ep', 'fsdp')
- output 6: float32 [896, 256], P('fsdp')
- output 7: float32 [256, 896], P(None, 'fsdp')
- output 8: float32 [896, 256], P('fsdp')
All inputs are finite; a program needn't handle non-finite values.
Results may differ from a plain program's by a relative error of at most 0.00489957.
Values are sent between devices in bfloat16 or wider.
A program may use at most 1 GiB of HBM per device.

v0:
```python
import jax
import jax.numpy as jnp
from jax import lax
from jax.sharding import PartitionSpec as P

CAP_NUM = 5
CAP_DEN = 4


def capacity_for(tok_dev, top_k, n_exp):
    needed = -(-(tok_dev * top_k * CAP_NUM) // (CAP_DEN * n_exp))
    return max(8, -(-needed // 8) * 8)


def route_slots(ids_dev, n_exp, capacity):
    flat_ids = ids_dev.reshape(-1)
    n_assign = flat_ids.shape[0]
    onehot = (flat_ids[:, None] == jnp.arange(n_exp, dtype=jnp.int32)[None, :]).astype(jnp.int32)
    slot_pos = jnp.sum(jnp.cumsum(onehot, axis=0) * onehot, axis=1) - 1
    slot_idx = jnp.where(slot_pos < capacity, flat_ids * capacity + slot_pos, n_exp * capacity)
    filled = jnp.full((n_exp * capacity + 1,), n_assign, jnp.int32)
    filled = filled.at[slot_idx].set(jnp.arange(n_assign, dtype=jnp.int32))
    return slot_idx, filled[: n_exp * capacity]


def swiglu_backward(x_rows, g_rows, w_a, w_b, w_c, lead_dims, batch_dim):
    up_form = lead_dims + "d," + batch_dim + "df->" + lead_dims + "f"
    back_form = lead_dims + "d," + batch_dim + "fd->" + lead_dims + "f"
    into_form = lead_dims + "f," + batch_dim + "df->" + lead_dims + "d"
    grad_in = lead_dims + "d," + lead_dims + "f->" + batch_dim + "df"
    grad_out = lead_dims + "f," + lead_dims + "d->" + batch_dim + "fd"
    h_one = jnp.einsum(up_form, x_rows, w_a, preferred_element_type=jnp.float32)
    h_three = jnp.einsum(up_form, x_rows, w_c, preferred_element_type=jnp.float32)
    sig_one = jax.nn.sigmoid(h_one)
    silu_one = h_one * sig_one
    act_rows = (silu_one * h_three).astype(jnp.bfloat16)
    d_act = jnp.einsum(back_form, g_rows, w_b, preferred_element_type=jnp.float32)
    dh_one = (d_act * h_three * sig_one * (1.0 + h_one * (1.0 - sig_one))).astype(jnp.bfloat16)
    dh_three = (d_act * silu_one).astype(jnp.bfloat16)
    dx_rows = (jnp.einsum(into_form, dh_one, w_a, preferred_element_type=jnp.float32) + jnp.einsum(into_form, dh_three, w_c, preferred_element_type=jnp.float32)).astype(jnp.bfloat16)
    dw_a = jnp.einsum(grad_in, x_rows, dh_one, preferred_element_type=jnp.float32)
    dw_b = jnp.einsum(grad_out, act_rows, g_rows, preferred_element_type=jnp.float32)
    dw_c = jnp.einsum(grad_in, x_rows, dh_three, preferred_element_type=jnp.float32)
    return dx_rows, act_rows, dw_a, dw_b, dw_c


def solution(mesh):
    ep_size = mesh.shape["ep"]
    tok_spec = P(("fsdp", "ep"), None)
    in_specs = (tok_spec, tok_spec, tok_spec, tok_spec, P("ep", "fsdp", None), P("ep", None, "fsdp"), P("ep", "fsdp", None), P("fsdp", None), P(None, "fsdp"), P("fsdp", None))
    out_specs = (tok_spec, tok_spec, P("ep", "fsdp", None), P("ep", None, "fsdp"), P("ep", "fsdp", None), P("fsdp", None), P(None, "fsdp"), P("fsdp", None))

    def device_step(x_loc, dy_loc, ids_loc, gate_loc, w_one, w_two, w_three, ws_one, ws_two, ws_three):
        tok_dev, top_k = ids_loc.shape
        model_dim = x_loc.shape[1]
        n_local = w_one.shape[0]
        n_exp = n_local * ep_size
        capacity = capacity_for(tok_dev, top_k, n_exp)
        slot_idx, filled = route_slots(ids_loc, n_exp, capacity)
        zero_row = jnp.zeros((1, model_dim), jnp.bfloat16)
        zero_one = jnp.zeros((1,), jnp.float32)
        tok_src = filled // top_k
        buf_shape = (ep_size, n_local, capacity, model_dim)
        x_send = jnp.concatenate([x_loc, zero_row])[tok_src].reshape(buf_shape)
        dy_send = jnp.concatenate([dy_loc, zero_row])[tok_src].reshape(buf_shape)
        gate_send = jnp.concatenate([gate_loc.reshape(-1), zero_one])[filled].reshape(buf_shape[:3])
        x_recv = lax.all_to_all(x_send, "ep", 0, 0, tiled=True)
        dy_recv = lax.all_to_all(dy_send, "ep", 0, 0, tiled=True)
        gate_recv = lax.all_to_all(gate_send, "ep", 0, 0, tiled=True)
        w_one_full = lax.all_gather(w_one, "fsdp", axis=1, tiled=True)
        w_three_full = lax.all_gather(w_three, "fsdp", axis=1, tiled=True)
        w_two_full = lax.all_gather(w_two, "fsdp", axis=2, tiled=True)
        ws_one_full = lax.all_gather(ws_one, "fsdp", axis=0, tiled=True)
        ws_three_full = lax.all_gather(ws_three, "fsdp", axis=0, tiled=True)
        ws_two_full = lax.all_gather(ws_two, "fsdp", axis=1, tiled=True)
        dy_wide = dy_recv.astype(jnp.float32)
        g_recv = (gate_recv[..., None] * dy_wide).astype(jnp.bfloat16)
        dx_recv, act_recv, dw_one, dw_two, dw_three = swiglu_backward(x_recv, g_recv, w_one_full, w_two_full, w_three_full, "sec", "e")
        y_recv = jnp.einsum("secf,efd->secd", act_recv, w_two_full, preferred_element_type=jnp.float32)
        dgate_recv = jnp.sum(dy_wide * y_recv, axis=-1)
        dx_back = lax.all_to_all(dx_recv, "ep", 0, 0, tiled=True).reshape(n_exp * capacity, model_dim)
        dgate_back = lax.all_to_all(dgate_recv, "ep", 0, 0, tiled=True).reshape(-1)
        dx_assign = jnp.concatenate([dx_back, zero_row])[slot_idx].reshape(tok_dev, top_k, model_dim)
        dgate_loc = jnp.concatenate([dgate_back, zero_one])[slot_idx].reshape(tok_dev, top_k)
        shared_out = swiglu_backward(x_loc, dy_loc, ws_one_full, ws_two_full, ws_three_full, "t", "")
        dx_loc = (jnp.sum(dx_assign.astype(jnp.float32), axis=1) + shared_out[0].astype(jnp.float32)).astype(jnp.bfloat16)
        dw_one = lax.psum_scatter(dw_one, "fsdp", scatter_dimension=1, tiled=True)
        dw_three = lax.psum_scatter(dw_three, "fsdp", scatter_dimension=1, tiled=True)
        dw_two = lax.psum_scatter(dw_two, "fsdp", scatter_dimension=2, tiled=True)
        dws_one = lax.psum(lax.psum_scatter(shared_out[2], "fsdp", scatter_dimension=0, tiled=True), "ep")
        dws_two = lax.psum(lax.psum_scatter(shared_out[3], "fsdp", scatter_dimension=1, tiled=True), "ep")
        dws_three = lax.psum(lax.psum_scatter(shared_out[4], "fsdp", scatter_dimension=0, tiled=True), "ep")
        return dx_loc, dgate_loc, dw_one, dw_two, dw_three, dws_one, dws_two, dws_three

    return jax.shard_map(device_step, mesh=mesh, in_specs=in_specs, out_specs=out_specs, check_vma=False)
```

profile of v0, /device:TPU:0, one launch (start us, length us, event | category | flops | bytes accessed | tf_op | source)
XLA Modules:
  0.0 4639.8 jit_solution(17170447534201237262)
XLA Ops:
  16.0 243.2 %fusion.21 = s32[256,256,128]{1,0,2:T(8,128)} fusion(s32[256,128]{0,1:T(8,128)S(1)} %copy.79), kind=kOutput, calls=%fused_computation.36 | output fusion | flops 1082130432 | bytes 33685504 | tf_op jit(solution)/shard_map/reduce-window
  260.9 24.3 broadcast_add_fusion
  285.2 34.2 copy.83
  319.4 12.0 fusion.20
  331.6 120.1 %scatter_custom_fusion = s32[40961]{0:T(1024)S(1)} fusion(s32[32768]{0:T(1024)S(1)} %bitcast.133, s32[32768]{0:T(1024)S(1)} %iota.11, s32[]{:T(128)} %constant.16.clone.1), kind=kCustom, calls=%fused_computation.83 | custom fusion | bytes 163848 | tf_op jit(solution)/shard_map/scatter | solution.py:22
  452.0 225.5 %gather_fusion = f32[40960]{0:T(1024)S(1)} fusion(f32[32769]{0:T(1024)S(1)} %pad_maximum_fusion.1, s32[40960]{0:T(1024)S(1)} %get-tuple-element.56), kind=kCustom, calls=%fused_computation | custom fusion | bytes 491520 | tf_op jit(solution)/shard_map/gather | solution.py:66
  689.7 193.0 %gather_fusion.2 = bf16[40960,896]{1,0:T(8,128)(2,1)} fusion(bf16[4097,896]{1,0:T(8,128)(2,1)} %concatenate.17, s32[40960]{0:T(1024)S(1)} %get-tuple-element.57), kind=kCustom, calls=%fused_computation.2 | custom fusion | bytes 146964480 | tf_op jit(solution)/shard_map/gather | solution.py:64
  882.7 14.1 all-to-all-start.2
  896.9 9.8 all_gather.23
  906.7 8.1 all_gather.22
  950.9 9.8 fusion.45
  968.6 193.1 %gather_fusion.1 = bf16[40960,896]{1,0:T(8,128)(2,1)} fusion(bf16[4097,896]{1,0:T(8,128)(2,1)} %concatenate.16, s32[40960]{0:T(1024)S(1)} %get-tuple-element.57), kind=kCustom, calls=%fused_computation.1 | custom fusion | bytes 146964480 | tf_op jit(solution)/shard_map/gather | solution.py:65
  1161.8 524.9 %all-to-all-done.2 = bf16[4,64,160,896]{3,2,1,0:T(8,128)(2,1)} async-done(((bf16[4,64,160,896]{3,2,1,0:T(8,128)(2,1)}), bf16[4,64,160,896]{3,2,1,0:T(8,128)(2,1)}, u32[]{:S(2)}, u32[]{:S(2)}) %all-to-all-start.2) | async-done | bytes 73400352 | tf_op jit(solution)/shard_map/all_to_all | solution.py:67
  1686.7 13.8 all-to-all-start.1
  1706.4 51.3 %fusion.3 = f32[64,4,160,256]{3,2,1,0:T(8,128)} fusion(bf16[4,64,160,896]{3,2,1,0:T(8,128)(2,1)} %all-to-all-done.2, bf16[64,896,256]{2,1,0:T(8,128)(2,1)} %all-gather.8.cloned.1.call-done), kind=kOutput, calls=%fused_computation.13 | convolution fusion | flops 18790481920 | bytes 144703488 | tf_op jit(solution)/shard_map/secd,edf->secf/dot_general | solution.py:32
  1757.6 756.5 %all-to-all-done.1 = bf16[4,64,160,896]{3,2,1,0:T(8,128)(2,1)} async-done(((bf16[4,64,160,896]{3,2,1,0:T(8,128)(2,1)}), bf16[4,64,160,896]{3,2,1,0:T(8,128)(2,1)}, u32[]{:S(2)}, u32[]{:S(2)}) %all-to-all-start.1) | async-done | bytes 73400352 | tf_op jit(solution)/shard_map/all_to_all | solution.py:68
  2514.1 51.4 %fusion.9 = f32[64,4,160,256]{3,2,1,0:T(8,128)} fusion(f32[4,64,160]{2,0,1:T(4,128)S(1)} %copy.85, bf16[4,64,160,896]{3,2,1,0:T(8,128)(2,1)} %all-to-all-done.1, bf16[64,256,896]{1,2,0:T(8,128)(2,1)} %all-gather.4.cloned.1.call-done), kind=kOutput, calls=%fused_computation.18 | convolution fusion | flops 18900582400 | bytes 144867328 | tf_op jit(solution)/shard_map/secd,efd->secf/dot_general | solution.py:37
  2565.5 80.8 %fusion.18 = (bf16[4,64,160,256]{3,2,0,1:T(8,128)(2,1)}, bf16[4,64,160,256]{3,2,0,1:T(8,128)(2,1)}, bf16[4,64,160,256]{3,2,0,1:T(8,128)(2,1)}) fusion(f32[64,4,160,256]{3,2,1,0:T(8,128)} %fusion.3, f32[64,4,160,256]{3,2,1,0:T(8,128)} %fusion.9, bf16[64,896,256]{2,1,0:T(8,128)(2,1)} %all-gather.6.cloned.1.call-done, bf16[4,64,160,896]{3,2,1,0:T(8,128)(2,1)} %all-to-all-done.2), kind=kOutput, calls=%fused_computation.31 | convolution fusion | flops 18947768320 | bytes 249561088 | tf_op jit(solution)/shard_map/secd,edf->secf/dot_general | solution.py:33
  2646.3 56.2 %fusion.40 = f32[64,256,896]{1,2,0:T(8,128)} fusion(bf16[4,64,160,256]{3,2,0,1:T(8,128)(2,1)} %get-tuple-element.51, f32[4,64,160]{2,0,1:T(4,128)S(1)} %copy.85, bf16[4,64,160,896]{3,2,1,0:T(8,128)(2,1)} %all-to-all-done.1), kind=kOutput, calls=%fused_computation.53 | convolution fusion | flops 18900582400 | bytes 153255936 | tf_op jit(solution)/shard_map/secf,secd->efd/dot_general | solution.py:42
  2702.6 53.6 %fusion.37 = f32[64,896,256]{2,1,0:T(8,128)} fusion(bf16[4,64,160,896]{3,2,1,0:T(8,128)(2,1)} %all-to-all-done.2, bf16[4,64,160,256]{3,2,0,1:T(8,128)(2,1)} %get-tuple-element.53), kind=kOutput, calls=%fused_computation.52 | convolution fusion | flops 18790481920 | bytes 153092096 | tf_op jit(solution)/shard_map/secd,secf->edf/dot_general | solution.py:43
  2756.3 53.3 %fusion.34 = f32[64,896,256]{2,1,0:T(8,128)} fusion(bf16[4,64,160,896]{3,2,1,0:T(8,128)(2,1)} %all-to-all-done.2, bf16[4,64,160,256]{3,2,0,1:T(8,128)(2,1)} %get-tuple-element.52), kind=kOutput, calls=%fused_computation.51 | convolution fusion | flops 18790481920 | bytes 153092096 | tf_op jit(solution)/shard_map/secd,secf->edf/dot_general | solution.py:41
  2809.6 40.2 fusion.1
  2854.7 66.6 %fusion.23 = f32[64,4,160,896]{3,2,1,0:T(8,128)} fusion(bf16[4,64,160,256]{3,2,0,1:T(8,128)(2,1)} %get-tuple-element.52, bf16[64,896,256]{2,1,0:T(8,128)(2,1)} %all-gather.8.cloned.1.call-done), kind=kOutput, calls=%fused_computation.40 | convolution fusion | flops 18790481920 | bytes 197132288 | tf_op jit(solution)/shard_map/secf,edf->secd/dot_general | solution.py:40
  2921.2 84.7 %fusion.2 = bf16[4,64,160,896]{3,2,0,1:T(8,128)(2,1)} fusion(f32[64,4,160,896]{3,2,1,0:T(8,128)} %fusion.23, bf16[4,64,160,256]{3,2,0,1:T(8,128)(2,1)} %get-tuple-element.53, bf16[64,896,256]{2,1,0:T(8,128)(2,1)} %all-gather.6.cloned.1.call-done), kind=kOutput, calls=%fused_computation.12 | convolution fusion | flops 18863882240 | bytes 270532608 | tf_op jit(solution)/shard_map/secf,edf->secd/dot_general | solution.py:40
  3006.0 48.7 %copy.89 = bf16[4,64,160,896]{3,2,1,0:T(8,128)(2,1)} copy(bf16[4,64,160,896]{3,2,0,1:T(8,128)(2,1)} %fusion.2) | data formatting | bytes 146800640 | tf_op jit(solution)/shard_map/convert_element_type | solution.py:40
  3054.7 14.1 all-to-all-start.3
  3081.7 180.5 %gather_fusion.4 = f32[32768]{0:T(1024)S(1)} fusion(f32[40961]{0:T(1024)S(1)} %pad_maximum_fusion, s32[32768]{0:T(1024)S(1)} %broadcast_clamp_fusion), kind=kCustom, calls=%fused_computation.4 | custom fusion | bytes 393216 | tf_op jit(solution)/shard_map/gather | solution.py:84
  3264.6 593.7 %all-to-all-done.3 = bf16[4,64,160,896]{3,2,1,0:T(8,128)(2,1)} async-done(((bf16[4,64,160,896]{3,2,1,0:T(8,128)(2,1)}), bf16[4,64,160,896]{3,2,1,0:T(8,128)(2,1)}, u32[]{:S(2)}, u32[]{:S(2)}) %all-to-all-start.3) | async-done | bytes 73400352 | tf_op jit(solution)/shard_map/all_to_all | solution.py:81
  3858.3 48.2 %concatenate.18 = bf16[40961,896]{1,0:T(8,128)(2,1)} pad(bf16[40960,896]{1,0:T(8,128)(2,1)} %bitcast.19, bf16[]{:T(256)} %constant.39.clone.1), padding=0_1x0_0 | pad | bytes 146802432 | tf_op jit(solution)/shard_map/concatenate | solution.py:83
  3906.5 583.1 %gather_fusion.3 = bf16[32768,896]{1,0:T(8,128)(2,1)} fusion(bf16[40961,896]{1,0:T(8,128)(2,1)} %concatenate.18, s32[32768]{0:T(1024)S(1)} %broadcast_clamp_fusion), kind=kCustom, calls=%fused_computation.3 | custom fusion | bytes 117571584 | tf_op jit(solution)/shard_map/gather | solution.py:83
  4489.5 128.5 %convert_reduce_fusion = f32[4096,896]{1,0:T(8,128)} fusion(bf16[32768,896]{1,0:T(8,128)(2,1)} %gather_fusion.3), kind=kLoop, calls=%fused_computation.11 | loop fusion | flops 55050240 | bytes 73400320 | tf_op jit(solution)/shard_map/reduce_sum | solution.py:86
  4618.1 13.9 add_convert_fusion.1
  (126 shorter events, 93.8 us)
Async XLA Ops:
  331.6 120.4 %copy-start.8 = (s32[32768,1]{0,1:T(1,128)}, s32[32768,1]{0,1:T(1,128)S(1)}, u32[]{:S(2)}) copy-start(s32[32768,1]{0,1:T(1,128)S(1)} %compare_select_fusion) | copy-start | bytes 393220
  678.4 204.3 %all-to-all-start = ((f32[4,64,160]{2,1,0:T(8,128)}), f32[4,64,160]{2,1,0:T(8,128)}, u32[]{:S(2)}, u32[]{:S(2)}) async-start(f32[4,64,160]{2,1,0:T(8,128)} %reshape.110), calls=%async_computation | async-start | bytes 524288 | tf_op jit(solution)/shard_map/all_to_all | solution.py:69
  882.7 14.2 copy-start.11
  882.7 24.0 copy-start.12
  882.7 32.1 copy-start.13
  882.7 804.0 %all-to-all-start.2 = ((bf16[4,64,160,896]{3,2,1,0:T(8,128)(2,1)}), bf16[4,64,160,896]{3,2,1,0:T(8,128)(2,1)}, u32[]{:S(2)}, u32[]{:S(2)}) async-start(bf16[4,64,160,896]{3,2,1,0:T(8,128)(2,1)} %bitcast.10), calls=%async_computation.2 | async-start | bytes 146800640 | tf_op jit(solution)/shard_map/all_to_all | solution.py:67
  896.8 805.4 %reduce-scatter.21.cloned.1.call-start = ((), (), s32[]{:S(2)}) async-start(), calls=%async_computation.19 | async-start | bytes 1376256
  896.9 38.1 slice-start.2
  906.7 21.2 copy-start.6
  914.8 13.2 copy-start.4
  922.3 12.7 slice-start.3
  927.9 10.8 copy-start.14
  927.9 12.1 slice-start
  938.7 22.0 copy-start
  943.7 760.5 %reduce-scatter.19.cloned.1.call-start = ((), (), s32[]{:S(2)}) async-start(), calls=%async_computation.18 | async-start | bytes 1376256
  950.5 755.8 %reduce-scatter.17.cloned.1.call-start = ((), (), s32[]{:S(2)}) async-start(), calls=%async_computation.17 | async-start | bytes 1376256 | tf_op jit(solution)/shard_map/reduce_scatter | solution.py:91
  960.8 745.6 %all-gather.8.cloned.1.call-start = ((), (), s32[]{:S(2)}) async-start(), calls=%async_computation.13 | async-start | bytes 44040192 | tf_op jit(solution)/shard_map/all_gather | solution.py:70
  961.3 796.3 %all-gather.4.cloned.1.call-start = ((), (), s32[]{:S(2)}) async-start(), calls=%async_computation.11 | async-start | bytes 44040192 | tf_op jit(solution)/shard_map/all_gather | solution.py:72
  1686.7 827.5 %all-to-all-start.1 = ((bf16[4,64,160,896]{3,2,1,0:T(8,128)(2,1)}), bf16[4,64,160,896]{3,2,1,0:T(8,128)(2,1)}, u32[]{:S(2)}, u32[]{:S(2)}) async-start(bf16[4,64,160,896]{3,2,1,0:T(8,128)(2,1)} %bitcast.6), calls=%async_computation.1 | async-start | bytes 146800640 | tf_op jit(solution)/shard_map/all_to_all | solution.py:68
  1700.5 865.0 %all-gather.6.cloned.1.call-start = ((), (), s32[]{:S(2)}) async-start(), calls=%async_computation.12 | async-start | bytes 44040192 | tf_op jit(solution)/shard_map/all_gather | solution.py:71
  1701.1 1375.5 %all-reduce.7.cloned.1.call-start = ((), (), s32[]{:S(2)}) async-start(), calls=%async_computation.20 | async-start | bytes 3014656 | tf_op jit(solution)/shard_map/psum | solution.py:90
  1706.3 2925.6 %reduce-scatter.13.cloned.1.call-start = ((), (), s32[]{:S(2)}) async-start(), calls=%async_computation.15 | async-start | bytes 88080384 | tf_op jit(solution)/shard_map/reduce_scatter | solution.py:89
  2702.6 1929.4 %reduce-scatter.15.cloned.1.call-start = ((), (), s32[]{:S(2)}) async-start(), calls=%async_computation.16 | async-start | bytes 88080384 | tf_op jit(solution)/shard_map/reduce_scatter | solution.py:88
  2756.2 1875.7 %reduce-scatter.11.cloned.1.call-start = ((), (), s32[]{:S(2)}) async-start(), calls=%async_computation.14 | async-start | bytes 88080384 | tf_op jit(solution)/shard_map/reduce_scatter | solution.py:87
  2850.6 204.1 %all-to-all-start.4 = ((f32[4,64,160]{2,1,0:T(8,128)}), f32[4,64,160]{2,1,0:T(8,128)}, u32[]{:S(2)}, u32[]{:S(2)}) async-start(f32[4,64,160]{2,1,0:T(8,128)} %copy.90), calls=%async_computation.4 | async-start | bytes 524288 | tf_op jit(solution)/shard_map/all_to_all | solution.py:82
  3054.7 14.2 copy-start.1
  3054.7 14.2 copy-start.7
  3054.7 21.8 copy-start.9
  3054.7 803.6 %all-to-all-start.3 = ((bf16[4,64,160,896]{3,2,1,0:T(8,128)(2,1)}), bf16[4,64,160,896]{3,2,1,0:T(8,128)(2,1)}, u32[]{:S(2)}, u32[]{:S(2)}) async-start(bf16[4,64,160,896]{3,2,1,0:T(8,128)(2,1)} %copy.89), calls=%async_computation.3 | async-start | bytes 146800640 | tf_op jit(solution)/shard_map/all_to_all | solution.py:81
  4489.5 128.5 %copy-start.3 = (bf16[4096,256]{1,0:T(8,128)(2,1)S(1)}, bf16[4096,256]{1,0:T(8,128)(2,1)}, u32[]{:S(2)}) copy-start(bf16[4096,256]{1,0:T(8,128)(2,1)} %copy-done.2) | copy-start | bytes 6291460
  4489.5 128.5 %copy-start.5 = (bf16[896,256]{1,0:T(8,128)(2,1)S(1)}, bf16[896,256]{1,0:T(8,128)(2,1)}, u32[]{:S(2)}) copy-start(bf16[896,256]{1,0:T(8,128)(2,1)} %copy-done.4) | copy-start | bytes 1376260
  4618.1 13.9 copy-start.10
  (3 other events, 10.2 us)
Sparse Core Ops, SparseCore 0:
  943.8 16.2 reduce-scatter.20
  962.9 16.0 reduce-scatter.18
  981.8 16.0 reduce-scatter.16
  999.3 339.2 all-gather.7
  1339.9 339.2 all-gather.3
  1702.5 341.5 all-gather.5
  2047.2 61.1 all-reduce.6
  2702.7 637.0 reduce-scatter.12
  3342.6 636.1 reduce-scatter.14
  3981.5 636.1 reduce-scatter.10
where the time goes:
time: 4660 us; the launch traced here: 4640 us
  waiting for transfers between devices  1880 us (40%)
  local copies, waits for them, and re-layouts  1670 us (36%)
  matrix products  593 us (13%)
  other arithmetic  410 us (9%)
  starting transfers between devices  51.5 us (1%)
    all_to_all x1, waiting for transfers between devices, device_step(): dy_recv = lax.all_to_all(dy_send, 'ep', 0, 0, tiled=True)  756 us
    all_to_all x1, waiting for transfers between devices, device_step(): lax.all_to_all(dx_recv, 'ep', 0, 0, tiled=True)  594 us
    gather x1, local copies, waits for them, and re-layouts, device_step(): jnp.concatenate([dx_back, zero_row])[slot_idx]  583 us
    all_to_all x1, waiting for transfers between devices, device_step(): x_recv = lax.all_to_all(x_send, 'ep', 0, 0, tiled=True)  525 us
    another operation x5, other arithmetic  268 us
    gather x1, local copies, waits for them, and re-layouts, device_step(): jnp.concatenate([gate_loc.reshape(-1), zero_one])[filled]  226 us
    gather x1, local copies, waits for them, and re-layouts, device_step(): dy_send = jnp.concatenate([dy_loc, zero_row])[tok_src].reshape(buf_shape)  193 us
    gather x1, local copies, waits for them, and re-layouts, device_step(): x_send = jnp.concatenate([x_loc, zero_row])[tok_src].reshape(buf_shape)  193 us
  transfers between devices with their start and end apart: 15, of which 3 were waited for; matrix products, arithmetic and copies ran while one was open for 43% of the time, Pallas kernels for 0%

commit v1 on v0

v1 whole, which is shorter than its diff:
```python
import functools
import jax
import jax.numpy as jnp
from jax import lax
from jax.experimental import pallas as pl
from jax.experimental.pallas import tpu as pltpu
from jax.sharding import PartitionSpec as P


BF = jnp.bfloat16
F32 = jnp.float32
LANE = 128
SUB = 8
CAP_NUM = 5
CAP_DEN = 4
N_GROUP = 8


def capacity_for(tok_dev, top_k, n_exp):
    needed = -(-(tok_dev * top_k * CAP_NUM) // (CAP_DEN * n_exp))
    return max(8, -(-needed // 8) * 8)


def gather_kernel(own, cap, chunk, start_ref, cnt_ref, tok_ref, gate_ref, x_hbm, d_hbm, *rest):
    n_out = 3 if own else 2
    outs = rest[-7 - n_out:-7]
    xtab, dtab, xtile, gtile, dtile, stage, sem = rest[-7:]
    tok_dev, width = x_hbm.shape
    n_col = width // LANE
    e = pl.program_id(0)
    n_chunk = tok_dev // chunk

    def copies(c, slot):
        rows = pl.ds(c * chunk, chunk)
        return (
            pltpu.make_async_copy(x_hbm.at[rows, :], stage.at[slot, 0], sem.at[slot, 0]),
            pltpu.make_async_copy(d_hbm.at[rows, :], stage.at[slot, 1], sem.at[slot, 1]),
        )

    @pl.when(e == 0)
    def _():
        for cp in copies(0, 0):
            cp.start()

        @pl.loop(0, n_chunk)
        def _(c):
            slot = lax.rem(c, 2)

            @pl.when(c + 1 < n_chunk)
            def _():
                for cp in copies(c + 1, 1 - slot):
                    cp.start()

            for cp in copies(c, slot):
                cp.wait()
            for which, tab in ((0, xtab), (1, dtab)):
                @pl.loop(0, chunk // 16)
                def _(r):
                    rows = stage[slot, which, pl.ds(pl.multiple_of(r * 16, 16), 16), :].astype(F32)
                    for half in range(2):
                        base = (c * chunk + r * 16 + half * SUB) * SUB
                        for j in range(n_col):
                            tab[pl.ds(base + j, SUB, stride=SUB), :] = rows[half * SUB:(half + 1) * SUB, j * LANE:(j + 1) * LANE]

    s0 = start_ref[e]
    n = cnt_ref[e]
    unroll = 16

    @pl.loop(0, pl.cdiv(n, unroll))
    def _(b):
        first = s0 + b * unroll
        for i in range(unroll):
            row = pl.multiple_of(tok_ref[first + i], SUB)
            gate = gate_ref[first + i]
            dst = pl.ds(pl.multiple_of((b * unroll + i) * SUB, SUB), SUB)
            xtile[dst, :] = xtab[pl.ds(row, SUB), :]
            drow = dtab[pl.ds(row, SUB), :]
            gtile[dst, :] = drow * gate
            if own:
                dtile[dst, :] = drow

    tiles = (xtile, gtile, dtile) if own else (xtile, gtile)
    for tile, out in zip(tiles, outs):
        @pl.loop(0, cap // 16)
        def _(r):
            pos = lax.broadcasted_iota(jnp.int32, (16, LANE), 0) + r * 16
            keep = pos < n
            for j in range(n_col):
                lo = tile[pl.ds(r * 16 * SUB + j, SUB, stride=SUB), :]
                hi = tile[pl.ds(r * 16 * SUB + SUB * SUB + j, SUB, stride=SUB), :]
                both = jnp.concatenate([lo, hi], axis=0)
                both = jnp.where(keep, both, 0.0).astype(BF)
                out[0, 0, pl.ds(pl.multiple_of(r * 16, 16), 16), j * LANE:(j + 1) * LANE] = both


def gather_call(plane, bufs, starts, counts, tok8, gates, x_loc, d_loc, n_src, cap, own):
    n_local = starts.shape[0]
    tok_dev, width = x_loc.shape
    chunk = min(512, tok_dev)
    smem = pl.BlockSpec(memory_space=pltpu.SMEM)
    anyspec = pl.BlockSpec(memory_space=pl.ANY)
    n_buf = 3 if own else 2
    shapes = [jax.ShapeDtypeStruct((n_local, n_src if i < 2 else n_src // 2, cap, width), BF) for i in range(n_buf)]
    out_specs = [pl.BlockSpec((1, 1, cap, width), lambda e: (e, plane, 0, 0)) for _ in range(n_buf)]
    scratch = [
        pltpu.VMEM((tok_dev * SUB, LANE), F32),
        pltpu.VMEM((tok_dev * SUB, LANE), F32),
        pltpu.VMEM((cap * SUB, LANE), F32),
        pltpu.VMEM((cap * SUB, LANE), F32),
        pltpu.VMEM((cap * SUB if own else SUB, LANE), F32),
        pltpu.VMEM((2, 2, chunk, width), BF),
        pltpu.SemaphoreType.DMA((2, 2)),
    ]
    args = [starts, counts, tok8, gates, x_loc, d_loc]
    return pl.pallas_call(
        functools.partial(gather_kernel, own, cap, chunk),
        grid=(n_local,),
        in_specs=[smem, smem, smem, smem, anyspec, anyspec] + [anyspec] * len(bufs),
        out_specs=out_specs,
        out_shape=shapes,
        scratch_shapes=scratch,
        input_output_aliases={6 + i: i for i in range(len(bufs))},
        compiler_params=pltpu.CompilerParams(vmem_limit_bytes=60 * 1024 * 1024),
        name="gather_own" if own else "gather_other",
        cost_estimate=pl.CostEstimate(flops=30_000_000_000, bytes_accessed=60_000_000, transcendentals=0),
    )(*args, *bufs)


def _dot(a, b):
    return jnp.dot(a, b, preferred_element_type=F32)


def _dot_t(a, b):
    return lax.dot_general(a, b, (((1,), (1,)), ((), ())), preferred_element_type=F32)


def _dot_tn(a, b):
    return lax.dot_general(a, b, (((0,), (0,)), ((), ())), preferred_element_type=F32)


def expert_kernel(n_dst, cap, half_ref, xs, gs, ds, w1, w3, w2, *rest):
    dx_outs = rest[:n_dst]
    dg_out, dw1_out, dw2_out, dw3_out, a_scr, dh_scr = rest[n_dst:]
    n_own = n_dst * cap
    rows_all, width = xs.shape[1], xs.shape[2]
    ff = w1.shape[2]
    mine = width // 2
    half = half_ref[0]
    lo = (mine // LANE) * LANE
    wide = width - lo
    off = mine - lo
    for blk in range(rows_all // n_own):
        rows = slice(blk * n_own, (blk + 1) * n_own)
        x = xs[0, rows, :]
        h1 = _dot(x, w1[0])
        h3 = _dot(x, w3[0])
        da = _dot(gs[0, rows, :], w2[0])
        sig = jax.nn.sigmoid(h1)
        silu = h1 * sig
        a_scr[rows, :] = (silu * h3).astype(BF)
        dh_scr[rows, :ff] = (da * h3 * sig * (1.0 + h1 * (1.0 - sig))).astype(BF)
        dh_scr[rows, ff:] = (da * silu).astype(BF)
        if blk == 0:
            dx = _dot_t(dh_scr[rows, :ff], w1[0]) + _dot_t(dh_scr[rows, ff:], w3[0])
            dxb = dx.astype(BF)
            for s in range(n_dst):
                dx_outs[s][0] = dxb[s * cap:(s + 1) * cap, :]
            prod = _dot_t(a_scr[rows, :], w2[0]) * ds[0].astype(F32)
            part = prod[:, :LANE]
            for j in range(1, width // LANE):
                part = part + prod[:, j * LANE:(j + 1) * LANE]
            for r in range(n_own // LANE):
                dg_out[0, :, r * LANE:(r + 1) * LANE] = jnp.sum(part[r * LANE:(r + 1) * LANE, :].T, axis=0, keepdims=True)
    start = pl.multiple_of(half * lo, LANE)
    xh = xs[0, :, pl.ds(start, wide)]
    gh = gs[0, :, pl.ds(start, wide)]
    dw13 = _dot_tn(xh, dh_scr[...])
    dw2 = _dot_tn(gh, a_scr[...])

    @pl.when(half == 0)
    def _():
        dw1_out[0] = dw13[:mine, :ff]
        dw3_out[0] = dw13[:mine, ff:]
        dw2_out[0] = dw2[:mine, :]

    @pl.when(half != 0)
    def _():
        dw1_out[0] = dw13[off:, :ff]
        dw3_out[0] = dw13[off:, ff:]
        dw2_out[0] = dw2[off:, :]


def expert_call(half, xs, gs, ds, w_all, base, bufs):
    n_grp, width, ff = w_all.shape[0] // 3, w_all.shape[1], w_all.shape[2]
    n_local, n_src, cap = xs.shape[:3]
    n_own = ds.shape[1]
    mine = width // 2
    xs = xs.reshape(n_local, n_src * cap, width)
    gs = gs.reshape(n_local, n_src * cap, width)
    ds = ds.reshape(n_local, n_own * cap, width)
    at = lambda e: (e + base, 0, 0)
    loc = lambda e: (e, 0, 0)
    in_specs = [
        pl.BlockSpec(memory_space=pltpu.SMEM),
        pl.BlockSpec((1, n_src * cap, width), at),
        pl.BlockSpec((1, n_src * cap, width), at),
        pl.BlockSpec((1, n_own * cap, width), at),
        pl.BlockSpec((1, width, ff), loc),
        pl.BlockSpec((1, width, ff), lambda e: (e + n_grp, 0, 0)),
        pl.BlockSpec((1, width, ff), lambda e: (e + 2 * n_grp, 0, 0)),
    ]
    out_specs = [pl.BlockSpec((1, cap, width), loc)] * n_own
    out_specs += [pl.BlockSpec((1, 1, n_own * cap), loc)] + [pl.BlockSpec((1, mine, ff), at)] * 3
    out_shape = [jax.ShapeDtypeStruct((n_grp, cap, width), BF)] * n_own
    out_shape += [jax.ShapeDtypeStruct((n_grp, 1, n_own * cap), F32)] + [jax.ShapeDtypeStruct((n_local, mine, ff), F32)] * 3
    args = [half, xs, gs, ds, w_all, w_all, w_all]
    n_alias = 0 if bufs is None else 3
    if bufs is not None:
        in_specs += [pl.BlockSpec(memory_space=pl.ANY)] * 3
        args += list(bufs)

    def body(*refs):
        expert_kernel(n_own, cap, *refs[:7], *refs[7 + n_alias:])

    flops = 2 * n_grp * width * ff * (3 * n_src * cap + 3 * n_own * cap + 3 * n_src * cap // 2)
    outs = pl.pallas_call(
        body,
        grid=(n_grp,),
        in_specs=in_specs,
        out_specs=out_specs,
        out_shape=out_shape,
        scratch_shapes=[pltpu.VMEM((n_src * cap, ff), BF), pltpu.VMEM((n_src * cap, 2 * ff), BF)],
        input_output_aliases={7 + i: n_own + 1 + i for i in range(n_alias)},
        compiler_params=pltpu.CompilerParams(vmem_limit_bytes=60 * 1024 * 1024),
        name="experts",
        cost_estimate=pl.CostEstimate(flops=flops, bytes_accessed=n_grp * 9_000_000, transcendentals=n_grp * n_src * cap * ff),
    )(*args)
    return outs[:n_own], outs[n_own], outs[n_own + 1:]


def combine_kernel(n_ep, base, first, last, n_rows, *refs):
    me_ref, start_ref, cnt_ref, asg_ref, dg_ref = refs[:5]
    rest = refs[5:]
    rows_hbm, rest = rest[:n_rows], rest[n_rows:]
    if not first:
        acc_in, rest = rest[0], rest[1:]
    if last:
        shared_ref, rest = rest[0], rest[1:]
        dx_out, dg_out, rest = rest[0], rest[1], rest[2:]
    else:
        acc_out, rest = rest[0], rest[1:]
    acc, tile, buf, sem, acc_sem = rest
    n_grp, cap, width = rows_hbm[0].shape
    n_col = width // LANE
    pitch = cap + SUB
    n_exp = start_ref.shape[0]
    n_local = n_exp // n_ep
    tok_rows = acc.shape[0]
    per = n_rows // n_ep * n_grp

    def fetch(i, slot, go):
        for k in range(n_rows):
            @pl.when(lax.div(i, n_grp) == k)
            def _():
                cp = pltpu.make_async_copy(rows_hbm[k].at[lax.rem(i, n_grp)], buf.at[slot], sem.at[slot])
                cp.start() if go else cp.wait()

    fetch(0, 0, True)
    if first:
        @pl.loop(0, tok_rows // 64)
        def _(r):
            acc[pl.ds(pl.multiple_of(r * 64, 64), 64), :] = jnp.zeros((64, LANE), F32)
    else:
        pltpu.make_async_copy(acc_in, acc, acc_sem).start()
        pltpu.make_async_copy(acc_in, acc, acc_sem).wait()
    tile[n_col * pitch:, :] = jnp.zeros((tile.shape[0] - n_col * pitch, LANE), F32)
    code = jnp.where(
        lax.broadcasted_iota(jnp.int32, (SUB, LANE), 0) == n_col,
        lax.broadcasted_iota(jnp.int32, (SUB, LANE), 1),
        -1,
    )

    @pl.loop(0, n_rows * n_grp)
    def _(i):
        slot = lax.rem(i, 2)

        @pl.when(i + 1 < n_rows * n_grp)
        def _():
            fetch(i + 1, 1 - slot, True)

        fetch(i, slot, False)
        e = jnp.bitwise_xor(me_ref[1], lax.div(i, per)) * n_local + base + lax.rem(i, per)

        @pl.loop(0, cap // 16)
        def _(r):
            for j in range(n_col):
                v = buf[slot, pl.ds(pl.multiple_of(r * 16, 16), 16), j * LANE:(j + 1) * LANE].astype(F32)
                tile[pl.ds(pl.multiple_of(j * pitch + r * 16, SUB), 16), :] = v

        s0 = start_ref[e]
        d0 = i * cap
        unroll = 16

        @pl.loop(0, pl.cdiv(cnt_ref[e], unroll))
        def _(b):
            pos = b * unroll
            for u in range(unroll):
                a = asg_ref[s0 + pos + u]
                row = tile[pl.ds(pos + u, SUB, stride=pitch), :]
                row = jnp.where(code == (a & (SUB - 1)), dg_ref[d0 + pos + u], row)
                dst = pl.ds(pl.multiple_of(a & -SUB, SUB), SUB)
                acc[dst, :] = acc[dst, :] + row

    if last:
        @pl.loop(0, tok_rows // (16 * SUB))
        def _(r):
            rows = pl.ds(pl.multiple_of(r * 16, 16), 16)
            both = []
            for j in range(n_col + 1):
                lo = acc[pl.ds(r * 16 * SUB + j, SUB, stride=SUB), :]
                hi = acc[pl.ds(r * 16 * SUB + SUB * SUB + j, SUB, stride=SUB), :]
                both.append(jnp.concatenate([lo, hi], axis=0))
            for j in range(n_col):
                col = slice(j * LANE, (j + 1) * LANE)
                dx_out[rows, col] = (both[j] + shared_ref[rows, col].astype(F32)).astype(BF)
            dg_out[rows, :] = both[n_col]
    else:
        pltpu.make_async_copy(acc, acc_out, acc_sem).start()
        pltpu.make_async_copy(acc, acc_out, acc_sem).wait()


def combine_call(place, starts, counts, asg, dg, rows, base, acc, shared, n_ep, tok_dev):
    n_rows = len(rows)
    first, last = acc is None, shared is not None
    _, cap, width = rows[0].shape
    smem = pl.BlockSpec(memory_space=pltpu.SMEM)
    anyspec = pl.BlockSpec(memory_space=pl.ANY)
    vmem = pl.BlockSpec(memory_space=pltpu.VMEM)
    args = [place, starts, counts, asg, dg, *rows]
    in_specs = [smem] * 5 + [anyspec] * n_rows
    if not first:
        args.append(acc)
        in_specs.append(anyspec)
    if last:
        args.append(shared)
        in_specs.append(vmem)
        out_shape = [jax.ShapeDtypeStruct((tok_dev, width), BF), jax.ShapeDtypeStruct((tok_dev, LANE), F32)]
        out_specs = [vmem, vmem]
    else:
        out_shape = jax.ShapeDtypeStruct((tok_dev * SUB, LANE), F32)
        out_specs = anyspec
    return pl.pallas_call(
        functools.partial(combine_kernel, n_ep, base, first, last, n_rows),
        in_specs=in_specs,
        out_specs=out_specs,
        out_shape=out_shape,
        scratch_shapes=[
            pltpu.VMEM((tok_dev * SUB, LANE), F32),
            pltpu.VMEM((SUB * (cap + SUB), LANE), F32),
            pltpu.VMEM((2, cap, width), BF),
            pltpu.SemaphoreType.DMA((2,)),
            pltpu.SemaphoreType.DMA,
        ],
        input_output_aliases={} if first or last else {5 + n_rows: 0},
        compiler_params=pltpu.CompilerParams(vmem_limit_bytes=60 * 1024 * 1024),
        name="combine",
        cost_estimate=pl.CostEstimate(flops=n_rows * 3_000_000_000, bytes_accessed=n_rows * 3_000_000, transcendentals=0),
    )(*args)


def sort_assignments(ids_dev, gate_dev, n_exp, cap):
    n_assign = ids_dev.size
    key = ids_dev.reshape(-1) * n_assign + jnp.arange(n_assign, dtype=jnp.int32)
    key, gates = lax.sort((key, gate_dev.reshape(-1)), num_keys=1)
    edges = jnp.arange(n_exp + 1, dtype=jnp.int32) * n_assign
    starts = jnp.sum((key[None, :] < edges[:, None]).astype(jnp.int32), axis=1)
    counts = jnp.minimum(starts[1:] - starts[:-1], cap)
    pad = 2 * LANE
    asg = jnp.pad(key & (n_assign - 1), (0, pad))
    return asg, jnp.pad(gates, (0, pad)), starts[:-1], counts


def shared_backward(x_rows, g_rows, w_a, w_b, w_c):
    h_one = _dot(x_rows, w_a)
    h_three = _dot(x_rows, w_c)
    sig_one = jax.nn.sigmoid(h_one)
    silu_one = h_one * sig_one
    act_rows = (silu_one * h_three).astype(BF)
    d_act = _dot_t(g_rows, w_b)
    dh_one = (d_act * h_three * sig_one * (1.0 + h_one * (1.0 - sig_one))).astype(BF)
    dh_three = (d_act * silu_one).astype(BF)
    dx_rows = (_dot_t(dh_one, w_a) + _dot_t(dh_three, w_c)).astype(BF)
    return dx_rows, _dot_tn(x_rows, dh_one), _dot_tn(act_rows, g_rows), _dot_tn(x_rows, dh_three)


def solution(mesh):
    ep_size = mesh.shape["ep"]
    rows_size = mesh.shape["fsdp"]
    tok_spec = P(("fsdp", "ep"), None)
    in_specs = (tok_spec, tok_spec, tok_spec, tok_spec, P("ep", "fsdp", None), P("ep", None, "fsdp"), P("ep", "fsdp", None), P("fsdp", None), P(None, "fsdp"), P("fsdp", None))
    out_specs = (tok_spec, tok_spec, P("ep", "fsdp", None), P("ep", None, "fsdp"), P("ep", "fsdp", None), P("fsdp", None), P(None, "fsdp"), P("fsdp", None))

    def swap_row(v):
        return lax.ppermute(v, "fsdp", [(i, rows_size - 1 - i) for i in range(rows_size)])

    def swap_ep(v, k):
        return lax.ppermute(v, "ep", [(i, i ^ k) for i in range(ep_size)])

    def device_step(x_loc, dy_loc, ids_loc, gate_loc, w_one, w_two, w_three, ws_one, ws_two, ws_three):
        tok_dev, top_k = ids_loc.shape
        n_local = w_one.shape[0]
        n_exp = n_local * ep_size
        n_src = ep_size * rows_size
        cap = capacity_for(tok_dev, top_k, n_exp)
        n_grp = max(1, n_local // N_GROUP)
        n_parts = n_local // n_grp
        me, row = lax.axis_index("ep"), lax.axis_index("fsdp")
        place = jnp.stack([row, me]).astype(jnp.int32)

        near = (x_loc, dy_loc)
        far = tuple(swap_row(v) for v in near)
        near_x = tuple(swap_ep(v, 2) for v in near)
        near_c = tuple(swap_ep(v, 1) for v in near)

        ws_one_full = lax.all_gather(ws_one, "fsdp", axis=0, tiled=True)
        ws_three_full = lax.all_gather(ws_three, "fsdp", axis=0, tiled=True)
        ws_two_full = lax.all_gather(ws_two, "fsdp", axis=1, tiled=True)
        shared = shared_backward(x_loc, dy_loc, ws_one_full, ws_two_full, ws_three_full)
        dws_one = lax.psum(lax.psum_scatter(shared[1], "fsdp", scatter_dimension=0, tiled=True), "ep")
        dws_two = lax.psum(lax.psum_scatter(shared[2], "fsdp", scatter_dimension=1, tiled=True), "ep")
        dws_three = lax.psum(lax.psum_scatter(shared[3], "fsdp", scatter_dimension=0, tiled=True), "ep")

        ids_loc, gate_loc, shared = lax.optimization_barrier((ids_loc, gate_loc, shared))
        asg, gates, starts, counts = sort_assignments(ids_loc, gate_loc, n_exp, cap)
        n_list = asg.shape[0]
        meta = jnp.concatenate([asg & -SUB, starts, counts])
        meta_all = lax.all_gather(meta, ("fsdp", "ep"), axis=0)
        gates_all = lax.all_gather(gates, ("fsdp", "ep"), axis=0)

        def gather(plane, bufs, x_src, dy_src):
            own = plane < ep_size
            if plane == 0:
                meta_s, gates_s = meta, gates
            else:
                src = jnp.bitwise_xor(me, plane % ep_size) + ep_size * (row if own else rows_size - 1 - row)
                meta_s = lax.dynamic_index_in_dim(meta_all, src, 0, keepdims=False)
                gates_s = lax.dynamic_index_in_dim(gates_all, src, 0, keepdims=False)
            starts_s = lax.dynamic_slice(meta_s, (n_list + me * n_local,), (n_local,))
            counts_s = lax.dynamic_slice(meta_s, (n_list + n_exp + me * n_local,), (n_local,))
            take = tuple(bufs) if own else tuple(bufs[:2])
            new = gather_call(plane, take, starts_s, counts_s, meta_s[:n_list], gates_s, x_src, dy_src, n_src, cap, own)
            return tuple(new) + tuple(bufs[len(new):])

        bufs = gather(0, (), *near)
        bufs = gather(1, bufs, *near_c)

        sums = (dws_one, dws_two, dws_three)
        w_one, w_two, w_three, far, bufs, sums = lax.optimization_barrier((w_one, w_two, w_three, far, bufs, sums))
        dws_one, dws_two, dws_three = sums
        w_two = jnp.swapaxes(w_two, 1, 2)
        w_grp = []
        for g in range(n_parts):
            part = slice(g * n_grp, (g + 1) * n_grp)
            w_grp.append(lax.all_gather(jnp.concatenate([w_one[part], w_three[part], w_two[part]]), "fsdp", axis=1, tiled=True))
        far_x = tuple(swap_ep(v, 2) for v in far)
        far_c = tuple(swap_ep(v, 1) for v in far)
        near_xc = tuple(swap_ep(v, 1) for v in near_x)
        far_xc = tuple(swap_ep(v, 1) for v in far_x)
        for plane, src in enumerate((near_x, near_xc, far, far_c, far_x, far_xc), 2):
            order = plane if plane < ep_size else (4, 5, 6, 7)[plane - ep_size]
            bufs = gather(order, bufs, *src)
        xs, gs, ds = bufs

        grads = None
        back_rows, part_dg = [], []
        for g, w_full in enumerate(w_grp):
            dx_g, dg_g, grads = expert_call(place, xs, gs, ds, w_full, g * n_grp, grads)
            back_rows.append([dx_g[0]] + [swap_ep(dx_g[k], k) for k in range(1, ep_size)])
            part_dg.append(dg_g.reshape(n_grp, ep_size, cap))

        acc = None
        cuts = sorted({0, 5 * n_parts // 8, 7 * n_parts // 8, n_parts})
        for lo, hi in zip(cuts[:-1], cuts[1:]):
            dg = jnp.concatenate(part_dg[lo:hi])
            dg = [dg[:, 0]] + [swap_ep(dg[:, k], k) for k in range(1, ep_size)]
            dg = jnp.concatenate([d.reshape(-1) for d in dg])
            rows = [back_rows[g][k] for k in range(ep_size) for g in range(lo, hi)]
            final = shared[0] if hi == n_parts else None
            acc = combine_call(place, starts, counts, asg, dg, rows, lo * n_grp, acc, final, ep_size, tok_dev)
        dx_loc, dg_tok = acc
        dw_one, dw_two, dw_three = grads
        return dx_loc, dg_tok[:, :top_k], dw_one, jnp.swapaxes(dw_two, 1, 2), dw_three, dws_one, dws_two, dws_three

    return jax.shard_map(device_step, mesh=mesh, in_specs=in_specs, out_specs=out_specs, check_vma=False)
```

time: 4660 us -> 2710 us (0.58)
  local copies, waits for them, and re-layouts: 1670 us -> 73.1 us
  Pallas kernels: 0 us -> 1150 us
  waiting for transfers between devices: 1880 us -> 1280 us
  matrix products: 593 us -> 41.2 us
  other arithmetic: 410 us -> 71.7 us
    all_to_all x5 -> x0, waiting for transfers between devices: 1880 us -> none  [the longest x1 756 us: device_step(): dy_recv = lax.all_to_all(dy_send, 'ep', 0, 0, tiled=True)]
    gather x5 -> x0, local copies, waits for them, and re-layouts: 1380 us -> none  [the longest x1 583 us: device_step(): jnp.concatenate([dx_back, zero_row])[slot_idx]]
    ppermute x0 -> x47, waiting for transfers between devices: none -> 1280 us  [the longest x45 1140 us: swap_ep(): return lax.ppermute(v, 'ep', [(i, i ^ k) for i in range(ep_size)])]
    pallas_call x0 -> x19, Pallas kernels: none -> 1150 us  [the longest x8 537 us: gather_call(): pl.pallas_call(functools.partial(gather_kernel, own, cap, chunk), grid=(n...]
    dot_general x17 -> x8, matrix products: 593 us -> 41.2 us  [the longest x3 21.6 us: _dot_t(): lax.dot_general(a, b, (((1,), (1,)), ((), ())), preferred_element_type=F32)]
    another operation x5 -> x1, other arithmetic: 268 us -> 0.61 us  [device_step(): place = jnp.stack([row, me]).astype(jnp.int32)]
    reduce_sum x2 -> x1, other arithmetic: 141 us -> 4.3 us  [sort_assignments(): starts = jnp.sum((key[None, :] < edges[:, None]).astype(jnp.int32), axis=1)]
    scatter x1 -> x0, local copies, waits for them, and re-layouts: 120 us -> none  [route_slots(): filled = filled.at[slot_idx].set(jnp.arange(n_assign, dtype=jnp.int32))]
  transfers between devices with their start and end apart: 15 -> 61, of which waited for: 3 -> 27; matrix products, arithmetic and copies ran while one was open for 43% -> 5% of each run, Pallas kernels for 0% -> 41%
where the time goes in v1:
time: 2710 us; the launch traced here: 2690 us
  waiting for transfers between devices  1280 us (47%)
  Pallas kernels  1150 us (42%)
  local copies, waits for them, and re-layouts  73.1 us (3%)
  other arithmetic  71.7 us (3%)
  matrix products  41.2 us (2%)
  starting transfers between devices  28.7 us (1%)
  blocking collectives  27.5 us (1%)
    ppermute x45, waiting for transfers between devices, swap_ep(): return lax.ppermute(v, 'ep', [(i, i ^ k) for i in range(ep_size)])  1140 us
    pallas_call x8, Pallas kernels, gather_call(): pl.pallas_call(functools.partial(gather_kernel, own, cap, chunk), grid=(n...  537 us
    pallas_call x8, Pallas kernels, expert_call(): pl.pallas_call(body, grid=(n_grp,), in_specs=in_specs, out_specs=out_spec...  370 us
    pallas_call x3, Pallas kernels, combine_call(): pl.pallas_call(functools.partial(combine_kernel, n_ep, base, first, last,...  241 us
    ppermute x2, waiting for transfers between devices, swap_row(): lax.ppermute(v, 'fsdp', [(i, rows_size - 1 - i) for i in range(rows_size)])  138 us
  transfers between devices with their start and end apart: 61, of which 27 were waited for; matrix products, arithmetic and copies ran while one was open for 5% of the time, Pallas kernels for 41%

profile of v1, /device:TPU:0, one launch (start us, length us, event | category | flops | bytes accessed | tf_op | source)
XLA Modules:
  0.0 2688.8 jit_solution(2236477525631142448)
XLA Ops:
  117.5 71.5 %gather_own.4 = (bf16[64,8,160,896]{3,2,1,0:T(8,128)(2,1)}, bf16[64,8,160,896]{3,2,1,0:T(8,128)(2,1)}, bf16[64,4,160,896]{3,2,1,0:T(8,128)(2,1)}) custom-call(s32[64]{0:T(128)} %get-tuple-element.308.start_ref, s32[64]{0:T(128)} %get-tuple-element.307.cnt_ref, s32[33024]{0:T(1024)} %copy-done.6, f32[33024]{0:T(1024)} %copy-done.7, bf16[4096,896]{1,0:T(8,128)(2,1)} %x_hbm.1, ...), custom_call_target="tpu_custom_call" | custom-call | flops 30000001024 | bytes 60000000 | tf_op jit(solution)/shard_map/gather_own/pallas_call | solution.py:115
  204.4 71.6 %gather_own.5 = (bf16[64,8,160,896]{3,2,1,0:T(8,128)(2,1)}, bf16[64,8,160,896]{3,2,1,0:T(8,128)(2,1)}, bf16[64,4,160,896]{3,2,1,0:T(8,128)(2,1)}) custom-call(s32[64]{0:T(128)} %get-tuple-element.300.start_ref, s32[64]{0:T(128)} %get-tuple-element.299.cnt_ref, ...), custom_call_target="tpu_custom_call", output_to_operand_aliasing={{0}: (6, {}), {1}: (7, {}), {2}: (8, {})} | custom-call | flops 30000001024 | bytes 60000000 | tf_op jit(solution)/shard_map/gather_own/pallas_call | solution.py:115
  276.0 138.4 %collective-permute-done.x_hbm = bf16[4096,896]{1,0:T(8,128)(2,1)} collective-permute-done((bf16[4096,896]{1,0:T(8,128)(2,1)}, bf16[4096,896]{1,0:T(8,128)(2,1)}, u32[]{:S(2)}, u32[]{:S(2)}) %collective-permute-start) | collective-permute-done | bytes 7340064 | tf_op jit(solution)/shard_map/ppermute | solution.py:404
  487.4 153.0 %collective-permute-done.12.d_hbm = bf16[4096,896]{1,0:T(8,128)(2,1)} collective-permute-done((bf16[4096,896]{1,0:T(8,128)(2,1)}, bf16[4096,896]{1,0:T(8,128)(2,1)}, u32[]{:S(2)}, u32[]{:S(2)}) %collective-permute-start.12) | collective-permute-done | bytes 7340064 | tf_op jit(solution)/shard_map/ppermute | solution.py:407
  642.5 155.3 %collective-permute-done.10.x_hbm = bf16[4096,896]{1,0:T(8,128)(2,1)} collective-permute-done((bf16[4096,896]{1,0:T(8,128)(2,1)}, bf16[4096,896]{1,0:T(8,128)(2,1)}, u32[]{:S(2)}, u32[]{:S(2)}) %collective-permute-start.10) | collective-permute-done | bytes 7340064 | tf_op jit(solution)/shard_map/ppermute | solution.py:407
  809.5 71.4 %gather_own.6 = (bf16[64,8,160,896]{3,2,1,0:T(8,128)(2,1)}, bf16[64,8,160,896]{3,2,1,0:T(8,128)(2,1)}, bf16[64,4,160,896]{3,2,1,0:T(8,128)(2,1)}) custom-call(s32[64]{0:T(128)} %get-tuple-element.290.start_ref, s32[64]{0:T(128)} %get-tuple-element.289.cnt_ref, ...), custom_call_target="tpu_custom_call", output_to_operand_aliasing={{0}: (6, {}), {1}: (7, {}), {2}: (8, {})} | custom-call | flops 30000001024 | bytes 60000000 | tf_op jit(solution)/shard_map/gather_own/pallas_call | solution.py:115
  880.9 74.1 %collective-permute-done.4.x_hbm = bf16[4096,896]{1,0:T(8,128)(2,1)} collective-permute-done((bf16[4096,896]{1,0:T(8,128)(2,1)}, bf16[4096,896]{1,0:T(8,128)(2,1)}, u32[]{:S(2)}, u32[]{:S(2)}) %collective-permute-start.4) | collective-permute-done | bytes 7340064 | tf_op jit(solution)/shard_map/ppermute | solution.py:407
  955.0 156.2 %collective-permute-done.6.d_hbm = bf16[4096,896]{1,0:T(8,128)(2,1)} collective-permute-done((bf16[4096,896]{1,0:T(8,128)(2,1)}, bf16[4096,896]{1,0:T(8,128)(2,1)}, u32[]{:S(2)}, u32[]{:S(2)}) %collective-permute-start.6) | collective-permute-done | bytes 7340064 | tf_op jit(solution)/shard_map/ppermute | solution.py:407
  1111.2 72.6 %gather_own.7 = (bf16[64,8,160,896]{3,2,1,0:T(8,128)(2,1)}, bf16[64,8,160,896]{3,2,1,0:T(8,128)(2,1)}, bf16[64,4,160,896]{3,2,1,0:T(8,128)(2,1)}) custom-call(s32[64]{0:T(128)} %get-tuple-element.292.start_ref, s32[64]{0:T(128)} %get-tuple-element.291.cnt_ref, ...), custom_call_target="tpu_custom_call", output_to_operand_aliasing={{0}: (6, {}), {1}: (7, {}), {2}: (8, {})} | custom-call | flops 30000001024 | bytes 60000000 | tf_op jit(solution)/shard_map/gather_own/pallas_call | solution.py:115
  1183.8 62.4 %gather_other.4 = (bf16[64,8,160,896]{3,2,1,0:T(8,128)(2,1)}, bf16[64,8,160,896]{3,2,1,0:T(8,128)(2,1)}) custom-call(s32[64]{0:T(128)} %get-tuple-element.294.start_ref, s32[64]{0:T(128)} %get-tuple-element.293.cnt_ref, s32[33024]{0:T(1024)} %slice_reduce_fusion.2.tok_ref, ...), custom_call_target="tpu_custom_call", output_to_operand_aliasing={{0}: (6, {}), {1}: (7, {})} | custom-call | flops 30000001024 | bytes 60000000 | tf_op jit(solution)/shard_map/gather_other/pallas_call | solution.py:115
  1246.3 63.3 %gather_other.5 = (bf16[64,8,160,896]{3,2,1,0:T(8,128)(2,1)}, bf16[64,8,160,896]{3,2,1,0:T(8,128)(2,1)}) custom-call(s32[64]{0:T(128)} %get-tuple-element.296.start_ref, s32[64]{0:T(128)} %get-tuple-element.295.cnt_ref, s32[33024]{0:T(1024)} %slice_reduce_fusion.3.tok_ref, ...), custom_call_target="tpu_custom_call", output_to_operand_aliasing={{0}: (6, {}), {1}: (7, {})} | custom-call | flops 30000001024 | bytes 60000000 | tf_op jit(solution)/shard_map/gather_other/pallas_call | solution.py:115
  1309.6 62.3 %gather_other.6 = (bf16[64,8,160,896]{3,2,1,0:T(8,128)(2,1)}, bf16[64,8,160,896]{3,2,1,0:T(8,128)(2,1)}) custom-call(s32[64]{0:T(128)} %get-tuple-element.298.start_ref, s32[64]{0:T(128)} %get-tuple-element.297.cnt_ref, s32[33024]{0:T(1024)} %slice_reduce_fusion.4.tok_ref, ...), custom_call_target="tpu_custom_call", output_to_operand_aliasing={{0}: (6, {}), {1}: (7, {})} | custom-call | flops 30000001024 | bytes 60000000 | tf_op jit(solution)/shard_map/gather_other/pallas_call | solution.py:115
  1371.9 62.2 %gather_other.7 = (bf16[64,8,160,896]{3,2,1,0:T(8,128)(2,1)}, bf16[64,8,160,896]{3,2,1,0:T(8,128)(2,1)}) custom-call(s32[64]{0:T(128)} %get-tuple-element.302.start_ref, s32[64]{0:T(128)} %get-tuple-element.301.cnt_ref, s32[33024]{0:T(1024)} %slice_reduce_fusion.6.tok_ref, ...), custom_call_target="tpu_custom_call", output_to_operand_aliasing={{0}: (6, {}), {1}: (7, {})} | custom-call | flops 30000001024 | bytes 60000000 | tf_op jit(solution)/shard_map/gather_other/pallas_call | solution.py:115
  1526.4 46.3 %experts.10 = (bf16[8,160,896]{2,1,0:T(8,128)(2,1)}, bf16[8,160,896]{2,1,0:T(8,128)(2,1)}, bf16[8,160,896]{2,1,0:T(8,128)(2,1)}, bf16[8,160,896]{2,1,0:T(8,128)(...) custom-call(s32[2]{0:T(128)} %pad_add_fusion.1.refs_0_, ...), custom_call_target="tpu_custom_call", output_to_operand_aliasing={{5}: (7, {}), {6}: (8, {}), {7}: (9, {})} | custom-call | flops 28185722880 | bytes 72000000 | tf_op jit(solution)/shard_map/experts/pallas_call | solution.py:226
  1572.8 46.2 %experts.11 = (bf16[8,160,896]{2,1,0:T(8,128)(2,1)}, bf16[8,160,896]{2,1,0:T(8,128)(2,1)}, bf16[8,160,896]{2,1,0:T(8,128)(2,1)}, bf16[8,160,896]{2,1,0:T(8,128)(...) custom-call(s32[2]{0:T(128)} %pad_add_fusion.1.refs_0_, ...), custom_call_target="tpu_custom_call", output_to_operand_aliasing={{5}: (7, {}), {6}: (8, {}), {7}: (9, {})} | custom-call | flops 28185722880 | bytes 72000000 | tf_op jit(solution)/shard_map/experts/pallas_call | solution.py:226
  1619.0 46.4 %experts.12 = (bf16[8,160,896]{2,1,0:T(8,128)(2,1)}, bf16[8,160,896]{2,1,0:T(8,128)(2,1)}, bf16[8,160,896]{2,1,0:T(8,128)(2,1)}, bf16[8,160,896]{2,1,0:T(8,128)(...) custom-call(s32[2]{0:T(128)} %pad_add_fusion.1.refs_0_, ...), custom_call_target="tpu_custom_call", output_to_operand_aliasing={{5}: (7, {}), {6}: (8, {}), {7}: (9, {})} | custom-call | flops 28185722880 | bytes 72000000 | tf_op jit(solution)/shard_map/experts/pallas_call | solution.py:226
  1665.4 46.2 %experts.13 = (bf16[8,160,896]{2,1,0:T(8,128)(2,1)}, bf16[8,160,896]{2,1,0:T(8,128)(2,1)}, bf16[8,160,896]{2,1,0:T(8,128)(2,1)}, bf16[8,160,896]{2,1,0:T(8,128)(...) custom-call(s32[2]{0:T(128)} %pad_add_fusion.1.refs_0_, ...), custom_call_target="tpu_custom_call", output_to_operand_aliasing={{5}: (7, {}), {6}: (8, {}), {7}: (9, {})} | custom-call | flops 28185722880 | bytes 72000000 | tf_op jit(solution)/shard_map/experts/pallas_call | solution.py:226
  1711.6 46.4 %experts.14 = (bf16[8,160,896]{2,1,0:T(8,128)(2,1)}, bf16[8,160,896]{2,1,0:T(8,128)(2,1)}, bf16[8,160,896]{2,1,0:T(8,128)(2,1)}, bf16[8,160,896]{2,1,0:T(8,128)(...) custom-call(s32[2]{0:T(128)} %pad_add_fusion.1.refs_0_, ...), custom_call_target="tpu_custom_call", output_to_operand_aliasing={{5}: (7, {}), {6}: (8, {}), {7}: (9, {})} | custom-call | flops 28185722880 | bytes 72000000 | tf_op jit(solution)/shard_map/experts/pallas_call | solution.py:226
  1760.8 46.3 %experts.15 = (bf16[8,160,896]{2,1,0:T(8,128)(2,1)}, bf16[8,160,896]{2,1,0:T(8,128)(2,1)}, bf16[8,160,896]{2,1,0:T(8,128)(2,1)}, bf16[8,160,896]{2,1,0:T(8,128)(...) custom-call(s32[2]{0:T(128)} %pad_add_fusion.1.refs_0_, ...), custom_call_target="tpu_custom_call", output_to_operand_aliasing={{5}: (7, {}), {6}: (8, {}), {7}: (9, {})} | custom-call | flops 28185722880 | bytes 72000000 | tf_op jit(solution)/shard_map/experts/pallas_call | solution.py:226
  1810.0 49.9 %collective-permute-done.15 = f32[8,160]{1,0:T(8,128)S(1)} collective-permute-done((f32[8,160]{1,0:T(8,128)S(1)}, f32[8,160]{1,0:T(8,128)S(1)}, u32[]{:S(2)}, u32[]{:S(2)}) %collective-permute-start.15) | collective-permute-done | bytes 5152 | tf_op jit(solution)/shard_map/ppermute | solution.py:407
  1885.3 47.5 %collective-permute-done.41.refs_19_ = bf16[8,160,896]{2,1,0:T(8,128)(2,1)} collective-permute-done((bf16[8,160,896]{2,1,0:T(8,128)(2,1)}, bf16[8,160,896]{2,1,0:T(8,128)(2,1)}, u32[]{:S(2)}, u32[]{:S(2)}) %collective-permute-start.41) | collective-permute-done | bytes 2293792 | tf_op jit(solution)/shard_map/ppermute | solution.py:407
  1932.8 48.2 %collective-permute-done.46.refs_24_ = bf16[8,160,896]{2,1,0:T(8,128)(2,1)} collective-permute-done((bf16[8,160,896]{2,1,0:T(8,128)(2,1)}, bf16[8,160,896]{2,1,0:T(8,128)(2,1)}, u32[]{:S(2)}, u32[]{:S(2)}) %collective-permute-start.46) | collective-permute-done | bytes 2293792 | tf_op jit(solution)/shard_map/ppermute | solution.py:407
  1983.1 48.0 %collective-permute-done.40.refs_18_ = bf16[8,160,896]{2,1,0:T(8,128)(2,1)} collective-permute-done((bf16[8,160,896]{2,1,0:T(8,128)(2,1)}, bf16[8,160,896]{2,1,0:T(8,128)(2,1)}, u32[]{:S(2)}, u32[]{:S(2)}) %collective-permute-start.40) | collective-permute-done | bytes 2293792 | tf_op jit(solution)/shard_map/ppermute | solution.py:407
  2031.1 48.2 %collective-permute-done.45.refs_23_ = bf16[8,160,896]{2,1,0:T(8,128)(2,1)} collective-permute-done((bf16[8,160,896]{2,1,0:T(8,128)(2,1)}, bf16[8,160,896]{2,1,0:T(8,128)(2,1)}, u32[]{:S(2)}, u32[]{:S(2)}) %collective-permute-start.45) | collective-permute-done | bytes 2293792 | tf_op jit(solution)/shard_map/ppermute | solution.py:407
  2081.4 48.0 %collective-permute-done.39.refs_17_ = bf16[8,160,896]{2,1,0:T(8,128)(2,1)} collective-permute-done((bf16[8,160,896]{2,1,0:T(8,128)(2,1)}, bf16[8,160,896]{2,1,0:T(8,128)(2,1)}, u32[]{:S(2)}, u32[]{:S(2)}) %collective-permute-start.39) | collective-permute-done | bytes 2293792 | tf_op jit(solution)/shard_map/ppermute | solution.py:407
  2129.4 48.2 %collective-permute-done.44.refs_22_ = bf16[8,160,896]{2,1,0:T(8,128)(2,1)} collective-permute-done((bf16[8,160,896]{2,1,0:T(8,128)(2,1)}, bf16[8,160,896]{2,1,0:T(8,128)(2,1)}, u32[]{:S(2)}, u32[]{:S(2)}) %collective-permute-start.44) | collective-permute-done | bytes 2293792 | tf_op jit(solution)/shard_map/ppermute | solution.py:407
  2227.7 48.2 %collective-permute-done.43.refs_21_ = bf16[8,160,896]{2,1,0:T(8,128)(2,1)} collective-permute-done((bf16[8,160,896]{2,1,0:T(8,128)(2,1)}, bf16[8,160,896]{2,1,0:T(8,128)(2,1)}, u32[]{:S(2)}, u32[]{:S(2)}) %collective-permute-start.43) | collective-permute-done | bytes 2293792 | tf_op jit(solution)/shard_map/ppermute | solution.py:407
  2278.0 48.0 %collective-permute-done.37.refs_15_ = bf16[8,160,896]{2,1,0:T(8,128)(2,1)} collective-permute-done((bf16[8,160,896]{2,1,0:T(8,128)(2,1)}, bf16[8,160,896]{2,1,0:T(8,128)(2,1)}, u32[]{:S(2)}, u32[]{:S(2)}) %collective-permute-start.37) | collective-permute-done | bytes 2293792 | tf_op jit(solution)/shard_map/ppermute | solution.py:407
  2327.0 47.2 %collective-permute-done.42.refs_20_ = bf16[8,160,896]{2,1,0:T(8,128)(2,1)} collective-permute-done((bf16[8,160,896]{2,1,0:T(8,128)(2,1)}, bf16[8,160,896]{2,1,0:T(8,128)(2,1)}, u32[]{:S(2)}, u32[]{:S(2)}) %collective-permute-start.42) | collective-permute-done | bytes 2293792 | tf_op jit(solution)/shard_map/ppermute | solution.py:407
  2375.6 134.9 %combine.3.refs_13_ = f32[32768,128]{1,0:T(8,128)} custom-call(s32[2]{0:T(128)} %pad_add_fusion.1.refs_0_, s32[256]{0:T(256)} %copy-done.28, s32[256]{0:T(256)} %copy-done.27, s32[33024]{0:T(1024)} %get-tuple-element.310.refs_3_, f32[25600]{0:T(1024)} %pad_maximum_fusion.8.refs_4_, bf16[8,160,896]{2,1,0:T(8,128)(2,1)} %get-tuple-element.185.refs_5_, ...), custom_call_target="tpu_custom_call" | custom-call | flops 60000002048 | bytes 60000000 | tf_op jit(solution)/shard_map/combine/pallas_call | solution.py:352
  2522.6 48.2 %collective-permute-done.27.refs_11_ = bf16[8,160,896]{2,1,0:T(8,128)(2,1)} collective-permute-done((bf16[8,160,896]{2,1,0:T(8,128)(2,1)}, bf16[8,160,896]{2,1,0:T(8,128)(2,1)}, u32[]{:S(2)}, u32[]{:S(2)}) %collective-permute-start.27) | collective-permute-done | bytes 2293792 | tf_op jit(solution)/shard_map/ppermute | solution.py:407
  2570.8 64.4 %combine.4.refs_9_ = f32[32768,128]{1,0:T(8,128)} custom-call(s32[2]{0:T(128)} %pad_add_fusion.1.refs_0_, s32[256]{0:T(256)} %copy-done.28, s32[256]{0:T(256)} %copy-done.27, s32[33024]{0:T(1024)} %get-tuple-element.310.refs_3_, f32[10240]{0:T(1024)} %pad_maximum_fusion.9.refs_4_, ...), custom_call_target="tpu_custom_call", output_to_operand_aliasing={{}: (13, {})} | custom-call | flops 24000000000 | bytes 24000000 | tf_op jit(solution)/shard_map/combine/pallas_call | solution.py:352
  (312 shorter events, 450.5 us)
Async XLA Ops:
  8.0 181.1 %reduce-scatter.12.cloned.1.call-start = ((), (), s32[]{:S(2)}) async-start(), calls=%async_computation.14 | async-start | bytes 1376256
  39.6 151.6 %reduce-scatter.10.cloned.1.call-start = ((), (), s32[]{:S(2)}) async-start(), calls=%async_computation.13 | async-start | bytes 1376256
  67.4 208.6 %collective-permute-start.1 = (bf16[4096,896]{1,0:T(8,128)(2,1)}, bf16[4096,896]{1,0:T(8,128)(2,1)}, u32[]{:S(2)}, u32[]{:S(2)}) collective-permute-start(bf16[4096,896]{1,0:T(8,128)(2,1)} %d_hbm.1), channel_id=1, source_target_pairs={{0,4},{4,0},{1,5},{5,1},{2,6},{6,2},{3,7},{7,3}} | collective-permute-start | bytes 22020104 | tf_op jit(solution)/shard_map/ppermute | solution.py:404
  70.1 344.3 %collective-permute-start = (bf16[4096,896]{1,0:T(8,128)(2,1)}, bf16[4096,896]{1,0:T(8,128)(2,1)}, u32[]{:S(2)}, u32[]{:S(2)}) collective-permute-start(bf16[4096,896]{1,0:T(8,128)(2,1)} %x_hbm.1), channel_id=1, source_target_pairs={{0,4},{4,0},{1,5},{5,1},{2,6},{6,2},{3,7},{7,3}} | collective-permute-start | bytes 22020104 | tf_op jit(solution)/shard_map/ppermute | solution.py:404
  116.8 159.2 %all-reduce.5.cloned.1.call-start = ((), (), s32[]{:S(2)}) async-start(), calls=%async_computation.16 | async-start | bytes 3145728 | tf_op jit(solution)/shard_map/psum | solution.py:429
  195.2 1239.0 %all-gather.29.cloned.1.call-start = ((), (), s32[]{:S(2)}) async-start(), calls=%async_computation.10 | async-start | bytes 16515072 | tf_op jit(solution)/shard_map/all_gather | solution.py:464
  447.1 1033.2 %all-gather.27.cloned.1.call-start = ((), (), s32[]{:S(2)}) async-start(), calls=%async_computation.9 | async-start | bytes 16515072 | tf_op jit(solution)/shard_map/all_gather | solution.py:464
  453.3 1073.2 %all-gather.25.cloned.1.call-start = ((), (), s32[]{:S(2)}) async-start(), calls=%async_computation.8 | async-start | bytes 16515072 | tf_op jit(solution)/shard_map/all_gather | solution.py:464
  460.0 1112.8 %all-gather.23.cloned.1.call-start = ((), (), s32[]{:S(2)}) async-start(), calls=%async_computation.7 | async-start | bytes 16515072 | tf_op jit(solution)/shard_map/all_gather | solution.py:464
  466.4 1152.6 %all-gather.21.cloned.1.call-start = ((), (), s32[]{:S(2)}) async-start(), calls=%async_computation.6 | async-start | bytes 16515072 | tf_op jit(solution)/shard_map/all_gather | solution.py:464
  472.7 1192.7 %all-gather.19.cloned.1.call-start = ((), (), s32[]{:S(2)}) async-start(), calls=%async_computation.5 | async-start | bytes 16515072 | tf_op jit(solution)/shard_map/all_gather | solution.py:464
  479.2 1232.5 %all-gather.17.cloned.1.call-start = ((), (), s32[]{:S(2)}) async-start(), calls=%async_computation.4 | async-start | bytes 16515072 | tf_op jit(solution)/shard_map/all_gather | solution.py:464
  479.2 161.2 %collective-permute-start.12 = (bf16[4096,896]{1,0:T(8,128)(2,1)}, bf16[4096,896]{1,0:T(8,128)(2,1)}, u32[]{:S(2)}, u32[]{:S(2)}) collective-permute-start(bf16[4096,896]{1,0:T(8,128)(2,1)} %d_hbm.1), channel_id=1, source_target_pairs={{0,2},{1,3},{2,0},{3,1},{4,6},{5,7},{6,4},{7,5}} | collective-permute-start | bytes 22020104 | tf_op jit(solution)/shard_map/ppermute | solution.py:407
  480.1 317.6 %collective-permute-start.10 = (bf16[4096,896]{1,0:T(8,128)(2,1)}, bf16[4096,896]{1,0:T(8,128)(2,1)}, u32[]{:S(2)}, u32[]{:S(2)}) collective-permute-start(bf16[4096,896]{1,0:T(8,128)(2,1)} %x_hbm.1), channel_id=1, source_target_pairs={{0,2},{1,3},{2,0},{3,1},{4,6},{5,7},{6,4},{7,5}} | collective-permute-start | bytes 22020104 | tf_op jit(solution)/shard_map/ppermute | solution.py:407
  487.3 1273.4 %all-gather.15.cloned.1.call-start = ((), (), s32[]{:S(2)}) async-start(), calls=%async_computation.3 | async-start | bytes 16515072 | tf_op jit(solution)/shard_map/all_gather | solution.py:464
  640.4 169.0 %collective-permute-start.13 = (bf16[4096,896]{1,0:T(8,128)(2,1)}, bf16[4096,896]{1,0:T(8,128)(2,1)}, u32[]{:S(2)}, u32[]{:S(2)}) collective-permute-start(bf16[4096,896]{1,0:T(8,128)(2,1)} %collective-permute-done.12.d_hbm), channel_id=1, source_target_pairs={{0,1},{1,0},{2,3},{3,2},{4,5},{5,4},{6,7},{7,6}} | collective-permute-start | bytes 22020104 | tf_op jit(solution)/shard_map/ppermute | solution.py:407
  640.4 314.6 %collective-permute-start.4 = (bf16[4096,896]{1,0:T(8,128)(2,1)}, bf16[4096,896]{1,0:T(8,128)(2,1)}, u32[]{:S(2)}, u32[]{:S(2)}) collective-permute-start(bf16[4096,896]{1,0:T(8,128)(2,1)} %collective-permute-done.x_hbm), channel_id=1, source_target_pairs={{0,2},{1,3},{2,0},{3,1},{4,6},{5,7},{6,4},{7,5}} | collective-permute-start | bytes 22020104 | tf_op jit(solution)/shard_map/ppermute | solution.py:407
  641.3 469.9 %collective-permute-start.6 = (bf16[4096,896]{1,0:T(8,128)(2,1)}, bf16[4096,896]{1,0:T(8,128)(2,1)}, u32[]{:S(2)}, u32[]{:S(2)}) collective-permute-start(bf16[4096,896]{1,0:T(8,128)(2,1)} %collective-permute-done.1.d_hbm), channel_id=1, source_target_pairs={{0,2},{1,3},{2,0},{3,1},{4,6},{5,7},{6,4},{7,5}} | collective-permute-start | bytes 22020104 | tf_op jit(solution)/shard_map/ppermute | solution.py:407
  797.7 313.5 %collective-permute-start.11 = (bf16[4096,896]{1,0:T(8,128)(2,1)}, bf16[4096,896]{1,0:T(8,128)(2,1)}, u32[]{:S(2)}, u32[]{:S(2)}) collective-permute-start(bf16[4096,896]{1,0:T(8,128)(2,1)} %collective-permute-done.10.x_hbm), channel_id=1, source_target_pairs={{0,1},{1,0},{2,3},{3,2},{4,5},{5,4},{6,7},{7,6}} | collective-permute-start | bytes 22020104 | tf_op jit(solution)/shard_map/ppermute | solution.py:407
  803.8 442.5 %collective-permute-start.8 = (bf16[4096,896]{1,0:T(8,128)(2,1)}, bf16[4096,896]{1,0:T(8,128)(2,1)}, u32[]{:S(2)}, u32[]{:S(2)}) collective-permute-start(bf16[4096,896]{1,0:T(8,128)(2,1)} %collective-permute-done.x_hbm), channel_id=1, source_target_pairs={{0,1},{1,0},{2,3},{3,2},{4,5},{5,4},{6,7},{7,6}} | collective-permute-start | bytes 22020104 | tf_op jit(solution)/shard_map/ppermute | solution.py:407
  809.4 436.8 %collective-permute-start.9 = (bf16[4096,896]{1,0:T(8,128)(2,1)}, bf16[4096,896]{1,0:T(8,128)(2,1)}, u32[]{:S(2)}, u32[]{:S(2)}) collective-permute-start(bf16[4096,896]{1,0:T(8,128)(2,1)} %collective-permute-done.1.d_hbm), channel_id=1, source_target_pairs={{0,1},{1,0},{2,3},{3,2},{4,5},{5,4},{6,7},{7,6}} | collective-permute-start | bytes 22020104 | tf_op jit(solution)/shard_map/ppermute | solution.py:407
  955.0 416.9 %collective-permute-start.5 = (bf16[4096,896]{1,0:T(8,128)(2,1)}, bf16[4096,896]{1,0:T(8,128)(2,1)}, u32[]{:S(2)}, u32[]{:S(2)}) collective-permute-start(bf16[4096,896]{1,0:T(8,128)(2,1)} %collective-permute-done.4.x_hbm), channel_id=1, source_target_pairs={{0,1},{1,0},{2,3},{3,2},{4,5},{5,4},{6,7},{7,6}} | collective-permute-start | bytes 22020104 | tf_op jit(solution)/shard_map/ppermute | solution.py:407
  1111.2 260.7 %collective-permute-start.7 = (bf16[4096,896]{1,0:T(8,128)(2,1)}, bf16[4096,896]{1,0:T(8,128)(2,1)}, u32[]{:S(2)}, u32[]{:S(2)}) collective-permute-start(bf16[4096,896]{1,0:T(8,128)(2,1)} %collective-permute-done.6.d_hbm), channel_id=1, source_target_pairs={{0,1},{1,0},{2,3},{3,2},{4,5},{5,4},{6,7},{7,6}} | collective-permute-start | bytes 22020104 | tf_op jit(solution)/shard_map/ppermute | solution.py:407
  1884.5 194.8 %collective-permute-start.45 = (bf16[8,160,896]{2,1,0:T(8,128)(2,1)}, bf16[8,160,896]{2,1,0:T(8,128)(2,1)}, u32[]{:S(2)}, u32[]{:S(2)}) collective-permute-start(bf16[8,160,896]{2,1,0:T(8,128)(2,1)} %get-tuple-element.203), channel_id=1, source_target_pairs={{0,3},{1,2},{2,1},{3,0},{4,7},{5,6},{6,5},{7,4}} | collective-permute-start | bytes 6881288 | tf_op jit(solution)/shard_map/ppermute | solution.py:407
  1982.0 195.6 %collective-permute-start.44 = (bf16[8,160,896]{2,1,0:T(8,128)(2,1)}, bf16[8,160,896]{2,1,0:T(8,128)(2,1)}, u32[]{:S(2)}, u32[]{:S(2)}) collective-permute-start(bf16[8,160,896]{2,1,0:T(8,128)(2,1)} %get-tuple-element.202), channel_id=1, source_target_pairs={{0,3},{1,2},{2,1},{3,0},{4,7},{5,6},{6,5},{7,4}} | collective-permute-start | bytes 6881288 | tf_op jit(solution)/shard_map/ppermute | solution.py:407
  2080.3 195.6 %collective-permute-start.43 = (bf16[8,160,896]{2,1,0:T(8,128)(2,1)}, bf16[8,160,896]{2,1,0:T(8,128)(2,1)}, u32[]{:S(2)}, u32[]{:S(2)}) collective-permute-start(bf16[8,160,896]{2,1,0:T(8,128)(2,1)} %get-tuple-element.201), channel_id=1, source_target_pairs={{0,3},{1,2},{2,1},{3,0},{4,7},{5,6},{6,5},{7,4}} | collective-permute-start | bytes 6881288 | tf_op jit(solution)/shard_map/ppermute | solution.py:407
  2178.6 195.6 %collective-permute-start.42 = (bf16[8,160,896]{2,1,0:T(8,128)(2,1)}, bf16[8,160,896]{2,1,0:T(8,128)(2,1)}, u32[]{:S(2)}, u32[]{:S(2)}) collective-permute-start(bf16[8,160,896]{2,1,0:T(8,128)(2,1)} %get-tuple-element.200), channel_id=1, source_target_pairs={{0,3},{1,2},{2,1},{3,0},{4,7},{5,6},{6,5},{7,4}} | collective-permute-start | bytes 6881288 | tf_op jit(solution)/shard_map/ppermute | solution.py:407
  2227.7 407.5 %collective-permute-start.17 = (bf16[8,160,896]{2,1,0:T(8,128)(2,1)}, bf16[8,160,896]{2,1,0:T(8,128)(2,1)S(1)}, u32[]{:S(2)}, u32[]{:S(2)}) collective-permute-start(bf16[8,160,896]{2,1,0:T(8,128)(2,1)} %get-tuple-element.167), channel_id=1, source_target_pairs={{0,1},{1,0},{2,3},{3,2},{4,5},{5,4},{6,7},{7,6}} | collective-permute-start | bytes 6881288 | tf_op jit(solution)/shard_map/ppermute | solution.py:407
  2275.9 359.3 %collective-permute-start.18 = (bf16[8,160,896]{2,1,0:T(8,128)(2,1)}, bf16[8,160,896]{2,1,0:T(8,128)(2,1)}, u32[]{:S(2)}, u32[]{:S(2)}) collective-permute-start(bf16[8,160,896]{2,1,0:T(8,128)(2,1)} %get-tuple-element.168), channel_id=1, source_target_pairs={{0,2},{1,3},{2,0},{3,1},{4,6},{5,7},{6,4},{7,5}} | collective-permute-start | bytes 6881288 | tf_op jit(solution)/shard_map/ppermute | solution.py:407
  2276.9 358.3 %collective-permute-start.19 = (bf16[8,160,896]{2,1,0:T(8,128)(2,1)}, bf16[8,160,896]{2,1,0:T(8,128)(2,1)}, u32[]{:S(2)}, u32[]{:S(2)}) collective-permute-start(bf16[8,160,896]{2,1,0:T(8,128)(2,1)} %get-tuple-element.169), channel_id=1, source_target_pairs={{0,3},{1,2},{2,1},{3,0},{4,7},{5,6},{6,5},{7,4}} | collective-permute-start | bytes 6881288 | tf_op jit(solution)/shard_map/ppermute | solution.py:407
  2326.0 196.6 %collective-permute-start.25 = (bf16[8,160,896]{2,1,0:T(8,128)(2,1)}, bf16[8,160,896]{2,1,0:T(8,128)(2,1)}, u32[]{:S(2)}, u32[]{:S(2)}) collective-permute-start(bf16[8,160,896]{2,1,0:T(8,128)(2,1)} %get-tuple-element.176), channel_id=1, source_target_pairs={{0,2},{1,3},{2,0},{3,1},{4,6},{5,7},{6,4},{7,5}} | collective-permute-start | bytes 6881288 | tf_op jit(solution)/shard_map/ppermute | solution.py:407
  2374.2 196.6 %collective-permute-start.27 = (bf16[8,160,896]{2,1,0:T(8,128)(2,1)}, bf16[8,160,896]{2,1,0:T(8,128)(2,1)}, u32[]{:S(2)}, u32[]{:S(2)}) collective-permute-start(bf16[8,160,896]{2,1,0:T(8,128)(2,1)} %get-tuple-element.178), channel_id=1, source_target_pairs={{0,3},{1,2},{2,1},{3,0},{4,7},{5,6},{6,5},{7,4}} | collective-permute-start | bytes 6881288 | tf_op jit(solution)/shard_map/ppermute | solution.py:407
  (67 other events, 6128.4 us)
Sparse Core Ops, SparseCore 0:
  39.7 17.9 reduce-scatter.11
  67.5 27.5 reduce-scatter.9
  97.8 26.1 reduce-scatter.13
  195.3 38.0 all-reduce.4
  447.2 133.0 all-gather.28
  581.7 132.3 all-gather.26
  715.6 132.3 all-gather.24
  849.5 132.3 all-gather.22
  983.5 132.3 all-gather.20
  1117.3 132.3 all-gather.18
  1251.2 132.3 all-gather.16
  1385.6 132.3 all-gather.14
Sparse Core Ops, SparseCore 1:
  110.8 27.0 all-gather.32
  139.5 22.4 all-gather.30

commit v2 on v1

v2 whole, which is shorter than its diff:
```python
import functools
import jax
import jax.numpy as jnp
from jax import lax
from jax.experimental import pallas as pl
from jax.experimental.pallas import tpu as pltpu
from jax.sharding import PartitionSpec as P


CAP_NUM = 5
CAP_DEN = 4
N_GROUP = 8
BF = jnp.bfloat16
F32 = jnp.float32
LANE = 128
SUB = 8
VMEM_LIMIT = 60 * 1024 * 1024


def capacity_for(tok_dev, top_k, n_exp):
    needed = -(-(tok_dev * top_k * CAP_NUM) // (CAP_DEN * n_exp))
    return max(8, -(-needed // 8) * 8)


def pitch_for(cap):
    return cap + 4


def gather_kernel(own, cap, chunk, start_ref, cnt_ref, tok_ref, gate_ref, x_hbm, d_hbm, *rest):
    n_out = 3 if own else 2
    outs = rest[-7 - n_out:-7]
    xtab, dtab, xtile, gtile, dtile, stage, sem = rest[-7:]
    tok_dev, width = x_hbm.shape
    n_col = width // LANE
    pitch = pitch_for(cap)
    e = pl.program_id(0)
    n_chunk = tok_dev // chunk

    def copies(c, slot):
        rows = pl.ds(c * chunk, chunk)
        return (
            pltpu.make_async_copy(x_hbm.at[rows, :], stage.at[slot, 0], sem.at[slot, 0]),
            pltpu.make_async_copy(d_hbm.at[rows, :], stage.at[slot, 1], sem.at[slot, 1]),
        )

    @pl.when(e == 0)
    def _():
        for cp in copies(0, 0):
            cp.start()

        @pl.loop(0, n_chunk)
        def _(c):
            slot = lax.rem(c, 2)

            @pl.when(c + 1 < n_chunk)
            def _():
                for cp in copies(c + 1, 1 - slot):
                    cp.start()

            for cp in copies(c, slot):
                cp.wait()

            @pl.loop(0, chunk // 16)
            def _(r):
                for which, tab in ((0, xtab), (1, dtab)):
                    rows = stage[slot, which, pl.ds(pl.multiple_of(r * 16, 16), 16), :].astype(F32)
                    for part in range(2):
                        base = (c * chunk + r * 16 + part * SUB) * n_col
                        for j in range(n_col):
                            tab[pl.ds(base + j, SUB, stride=n_col), :] = rows[part * SUB:(part + 1) * SUB, j * LANE:(j + 1) * LANE]

    s0 = start_ref[e]
    n = cnt_ref[e]
    unroll = 16

    @pl.loop(0, pl.cdiv(n, unroll))
    def _(b):
        first = b * unroll
        for i in range(unroll):
            row = tok_ref[s0 + first + i]
            gate = gate_ref[s0 + first + i]
            dst = pl.ds(first + i, SUB, stride=pitch)
            xtile[dst, :] = xtab[pl.ds(row, SUB), :]
            drow = dtab[pl.ds(row, SUB), :]
            gtile[dst, :] = drow * gate
            if own:
                dtile[dst, :] = drow

    tiles = (xtile, gtile, dtile) if own else (xtile, gtile)

    @pl.loop(0, cap // 16)
    def _(r):
        pos = lax.broadcasted_iota(jnp.int32, (16, LANE), 0) + r * 16
        keep = pos < n
        for tile, out in zip(tiles, outs):
            view = tile.at[pl.ds(pl.multiple_of(r * 16, 16), (n_col - 1) * pitch + 16), :]
            for j in range(n_col):
                both = jnp.where(keep, view[j * pitch:j * pitch + 16, :], 0.0).astype(BF)
                out[0, 0, pl.ds(pl.multiple_of(r * 16, 16), 16), j * LANE:(j + 1) * LANE] = both


def gather_call(plane, bufs, starts, counts, toks, gates, x_loc, d_loc, n_src, cap, own):
    n_local = starts.shape[0]
    tok_dev, width = x_loc.shape
    n_col = width // LANE
    chunk = min(512, tok_dev)
    smem = pl.BlockSpec(memory_space=pltpu.SMEM)
    anyspec = pl.BlockSpec(memory_space=pl.ANY)
    n_buf = 3 if own else 2
    table = pltpu.VMEM((tok_dev * n_col + SUB, LANE), F32)
    tile = pltpu.VMEM((SUB * pitch_for(cap), LANE), F32)
    return pl.pallas_call(
        functools.partial(gather_kernel, own, cap, chunk),
        grid=(n_local,),
        in_specs=[smem, smem, smem, smem, anyspec, anyspec] + [anyspec] * len(bufs),
        out_specs=[pl.BlockSpec((1, 1, cap, width), lambda e: (e, plane, 0, 0)) for _ in range(n_buf)],
        out_shape=[jax.ShapeDtypeStruct((n_local, n_src if i < 2 else n_src // 2, cap, width), BF) for i in range(n_buf)],
        scratch_shapes=[
            table,
            table,
            tile,
            tile,
            tile if own else pltpu.VMEM((SUB, LANE), F32),
            pltpu.VMEM((2, 2, chunk, width), BF),
            pltpu.SemaphoreType.DMA((2, 2)),
        ],
        input_output_aliases={6 + i: i for i in range(len(bufs))},
        compiler_params=pltpu.CompilerParams(vmem_limit_bytes=VMEM_LIMIT),
        name="gather_own" if own else "gather_other",
        cost_estimate=pl.CostEstimate(flops=30_000_000_000, bytes_accessed=60_000_000, transcendentals=0),
    )(starts, counts, toks, gates, x_loc, d_loc, *bufs)


def _dot(a, b):
    return jnp.dot(a, b, preferred_element_type=F32)


def _dot_t(a, b):
    return lax.dot_general(a, b, (((1,), (1,)), ((), ())), preferred_element_type=F32)


def _dot_tn(a, b):
    return lax.dot_general(a, b, (((0,), (0,)), ((), ())), preferred_element_type=F32)


def expert_kernel(own, add, n_dst, cap, base, place_ref, xs, gs, *rest):
    if own:
        ds, rest = rest[0], rest[1:]
    w_mine, w_far, rest = rest[:3], rest[3:6], rest[6:]
    if add:
        dw_in, rest = rest[:3], rest[3:]
    if own:
        dx_outs, dg_outs, rest = rest[-7 - 2 * n_dst:-7 - n_dst], rest[-7 - n_dst:-7], rest[-7:]
    dw_outs = rest[-7:-4]
    wbuf, wsem, a_scr, dh_scr = rest[-4:]
    n_own = n_dst * cap
    rows_all, width = xs.shape[1], xs.shape[2]
    ff = wbuf.shape[3]
    mine = width // 2
    half = place_ref[0]
    lo = (mine // LANE) * LANE
    wide = width - lo
    off = mine - lo
    e, n_grp = pl.program_id(0), pl.num_programs(0)
    slot = lax.rem(e, 2)

    def weights(step, at):
        copies = []
        for k in range(3):
            here = pl.ds(pl.multiple_of(half * mine, mine), mine)
            there = pl.ds(pl.multiple_of((1 - half) * mine, mine), mine)
            copies.append(pltpu.make_async_copy(w_mine[k].at[base + step], wbuf.at[at, k, here, :], wsem.at[at, k, 0]))
            copies.append(pltpu.make_async_copy(w_far[k].at[step], wbuf.at[at, k, there, :], wsem.at[at, k, 1]))
        return copies

    @pl.when(e == 0)
    def _():
        for cp in weights(0, 0):
            cp.start()

    @pl.when(e + 1 < n_grp)
    def _():
        for cp in weights(e + 1, 1 - slot):
            cp.start()

    for cp in weights(e, slot):
        cp.wait()
    w1, w3, w2 = wbuf.at[slot, 0], wbuf.at[slot, 1], wbuf.at[slot, 2]

    for blk in range(rows_all // n_own):
        rows = slice(blk * n_own, (blk + 1) * n_own)
        x = xs[0, rows, :]
        h1 = _dot(x, w1[...])
        h3 = _dot(x, w3[...])
        da = _dot(gs[0, rows, :], w2[...])
        sig = jax.nn.sigmoid(h1)
        silu = h1 * sig
        a_scr[rows, :] = (silu * h3).astype(BF)
        dh_scr[rows, :ff] = (da * h3 * sig * (1.0 + h1 * (1.0 - sig))).astype(BF)
        dh_scr[rows, ff:] = (da * silu).astype(BF)
        if own and blk == 0:
            dx = _dot_t(dh_scr[rows, :ff], w1[...]) + _dot_t(dh_scr[rows, ff:], w3[...])
            dxb = dx.astype(BF)
            for s in range(n_dst):
                dx_outs[s][0] = dxb[s * cap:(s + 1) * cap, :]
            prod = _dot_t(a_scr[rows, :], w2[...]) * ds[0].astype(F32)
            part = prod[:, :LANE]
            for j in range(1, width // LANE):
                part = part + prod[:, j * LANE:(j + 1) * LANE]
            dgate = [jnp.sum(part[r * LANE:(r + 1) * LANE, :].T, axis=0, keepdims=True) for r in range(n_own // LANE)]
            dgate = jnp.concatenate(dgate, axis=1)
            for s in range(n_dst):
                dg_outs[s][0, :, :cap] = dgate[:, s * cap:(s + 1) * cap]
    start = pl.multiple_of(half * lo, LANE)
    xh = xs[0, :, pl.ds(start, wide)]
    gh = gs[0, :, pl.ds(start, wide)]
    dw13 = _dot_tn(xh, dh_scr[...])
    dw2 = _dot_tn(gh, a_scr[...])

    def write(first):
        keep = slice(first, first + mine)
        for out, val, k in zip(dw_outs, (dw13[keep, :ff], dw2[keep, :], dw13[keep, ff:]), range(3)):
            out[0] = val + dw_in[k][0] if add else val

    @pl.when(half == 0)
    def _():
        write(0)

    @pl.when(half != 0)
    def _():
        write(off)


def expert_call(rows, place, xs, gs, ds, w_mine, w_far, base, bufs):
    n_grp, mine, ff = w_far[0].shape
    n_local, n_src, cap, width = xs.shape
    n_dst = ds.shape[1]
    own, add = rows != "other", rows == "other"
    n_rows = n_src * cap if rows == "all" else n_dst * cap
    xs = xs.reshape(n_local, n_src * cap, width)
    gs = gs.reshape(n_local, n_src * cap, width)
    ds = ds.reshape(n_local, n_dst * cap, width)
    at = lambda e: (e + base, 0, 0)
    loc = lambda e: (e, 0, 0)
    src = lambda e: (e + base, 1 if add else 0, 0)
    anyspec = pl.BlockSpec(memory_space=pl.ANY)
    args = [place, xs, gs] + ([ds] if own else []) + list(w_mine) + list(w_far)
    in_specs = [pl.BlockSpec(memory_space=pltpu.SMEM)] + [pl.BlockSpec((1, n_rows, width), src)] * 2
    in_specs += [pl.BlockSpec((1, n_dst * cap, width), at)] * own + [anyspec] * 6
    n_in = len(args)
    if bufs is not None:
        args += list(bufs)
        in_specs += [pl.BlockSpec((1, mine, ff), at) if add else anyspec] * 3
    out_specs, out_shape = [], []
    if own:
        line = pl.cdiv(cap, LANE) * LANE
        out_specs += [pl.BlockSpec((1, cap, width), loc)] * n_dst + [pl.BlockSpec((1, 1, line), loc)] * n_dst
        out_shape += [jax.ShapeDtypeStruct((n_grp, cap, width), BF)] * n_dst + [jax.ShapeDtypeStruct((n_grp, 1, line), F32)] * n_dst
    n_out = len(out_shape)
    out_specs += [pl.BlockSpec((1, mine, ff), at)] * 3
    out_shape += [jax.ShapeDtypeStruct((n_local, mine, ff), F32)] * 3
    units = {"all": 3 * n_src + 3 * n_dst + 3 * n_src // 2, "own": 6 * n_dst + 3 * n_dst // 2, "other": 3 * n_dst + 3 * n_dst // 2}[rows]
    outs = pl.pallas_call(
        functools.partial(expert_kernel, own, add, n_dst, cap, base),
        grid=(n_grp,),
        in_specs=in_specs,
        out_specs=out_specs,
        out_shape=out_shape,
        scratch_shapes=[
            pltpu.VMEM((2, 3, width, ff), BF),
            pltpu.SemaphoreType.DMA((2, 3, 2)),
            pltpu.VMEM((n_rows, ff), BF),
            pltpu.VMEM((n_rows, 2 * ff), BF),
        ],
        input_output_aliases={} if bufs is None else {n_in + i: n_out + i for i in range(3)},
        compiler_params=pltpu.CompilerParams(vmem_limit_bytes=VMEM_LIMIT),
        cost_estimate=pl.CostEstimate(flops=2 * n_grp * width * ff * units * cap, bytes_accessed=n_grp * 9_000_000, transcendentals=n_grp * n_rows * ff),
    )(*args)
    return (outs[:n_dst], outs[n_dst:n_out], outs[n_out:]) if own else outs


def combine_kernel(n_ep, base, first, last, n_rows, *refs):
    place_ref, start_ref, cnt_ref, asg_ref = refs[:4]
    rows_hbm, dg_hbm, rest = refs[4:4 + n_rows], refs[4 + n_rows:4 + 2 * n_rows], refs[4 + 2 * n_rows:]
    if not first:
        acc_in, rest = rest[0], rest[1:]
    if last:
        shared_ref, rest = rest[0], rest[1:]
        dx_out, dg_out, rest = rest[0], rest[1], rest[2:]
    else:
        acc_out, rest = rest[0], rest[1:]
    acc, tile, buf, dg_buf, sem, acc_sem = rest
    n_grp, cap, width = rows_hbm[0].shape
    n_col = width // LANE
    pitch = pitch_for(cap)
    n_exp = start_ref.shape[0]
    n_local = n_exp // n_ep
    tok_rows = acc.shape[0]
    per = n_rows // n_ep * n_grp
    unroll = 16

    def fetch(i, slot, go):
        for k in range(n_rows):
            @pl.when(lax.div(i, n_grp) == k)
            def _():
                for c, (src, dst) in enumerate(((rows_hbm[k], buf), (dg_hbm[k], dg_buf))):
                    cp = pltpu.make_async_copy(src.at[lax.rem(i, n_grp)], dst.at[slot], sem.at[slot, c])
                    cp.start() if go else cp.wait()

    fetch(0, 0, True)
    if first:
        @pl.loop(0, tok_rows // 64)
        def _(r):
            acc[pl.ds(pl.multiple_of(r * 64, 64), 64), :] = jnp.zeros((64, LANE), F32)
    else:
        pltpu.make_async_copy(acc_in, acc, acc_sem).start()
        pltpu.make_async_copy(acc_in, acc, acc_sem).wait()
    tile[n_col * pitch:, :] = jnp.zeros((tile.shape[0] - n_col * pitch, LANE), F32)
    code = jnp.where(
        lax.broadcasted_iota(jnp.int32, (SUB, LANE), 0) == n_col,
        lax.broadcasted_iota(jnp.int32, (SUB, LANE), 1),
        -1,
    )

    @pl.loop(0, n_rows * n_grp)
    def _(i):
        slot = lax.rem(i, 2)

        @pl.when(i + 1 < n_rows * n_grp)
        def _():
            fetch(i + 1, 1 - slot, True)

        fetch(i, slot, False)
        e = jnp.bitwise_xor(place_ref[1], lax.div(i, per)) * n_local + base + lax.rem(i, per)
        blocks = pl.cdiv(cnt_ref[e], unroll)

        @pl.loop(0, blocks)
        def _(r):
            view = tile.at[pl.ds(pl.multiple_of(r * 16, 16), (n_col - 1) * pitch + 16), :]
            for j in range(n_col):
                v = buf[slot, pl.ds(pl.multiple_of(r * 16, 16), 16), j * LANE:(j + 1) * LANE].astype(F32)
                view[j * pitch:j * pitch + 16, :] = v

        s0 = start_ref[e]

        @pl.loop(0, blocks)
        def _(b):
            pos = b * unroll
            for u in range(unroll):
                a = asg_ref[s0 + pos + u]
                row = tile[pl.ds(pos + u, SUB, stride=pitch), :]
                row = jnp.where(code == (a & (SUB - 1)), dg_buf[slot, 0, pos + u], row)
                dst = pl.ds(pl.multiple_of(a & -SUB, SUB), SUB)
                acc[dst, :] = acc[dst, :] + row

    if last:
        @pl.loop(0, tok_rows // (16 * SUB))
        def _(r):
            rows = pl.ds(pl.multiple_of(r * 16, 16), 16)
            both = []
            for j in range(n_col + 1):
                lo = acc[pl.ds(r * 16 * SUB + j, SUB, stride=SUB), :]
                hi = acc[pl.ds(r * 16 * SUB + SUB * SUB + j, SUB, stride=SUB), :]
                both.append(jnp.concatenate([lo, hi], axis=0))
            for j in range(n_col):
                col = slice(j * LANE, (j + 1) * LANE)
                dx_out[rows, col] = (both[j] + shared_ref[rows, col].astype(F32)).astype(BF)
            dg_out[rows, :] = both[n_col]
    else:
        pltpu.make_async_copy(acc, acc_out, acc_sem).start()
        pltpu.make_async_copy(acc, acc_out, acc_sem).wait()


def combine_call(place, starts, counts, asg, dg, rows, base, acc, shared, n_ep, tok_dev):
    n_rows = len(rows)
    first, last = acc is None, shared is not None
    _, cap, width = rows[0].shape
    smem = pl.BlockSpec(memory_space=pltpu.SMEM)
    anyspec = pl.BlockSpec(memory_space=pl.ANY)
    vmem = pl.BlockSpec(memory_space=pltpu.VMEM)
    args = [place, starts, counts, asg, *rows, *dg]
    in_specs = [smem] * 4 + [anyspec] * (2 * n_rows)
    if not first:
        args.append(acc)
        in_specs.append(anyspec)
    if last:
        args.append(shared)
        in_specs.append(vmem)
        out_shape = [jax.ShapeDtypeStruct((tok_dev, width), BF), jax.ShapeDtypeStruct((tok_dev, LANE), F32)]
        out_specs = [vmem, vmem]
    else:
        out_shape = jax.ShapeDtypeStruct((tok_dev * SUB, LANE), F32)
        out_specs = anyspec
    return pl.pallas_call(
        functools.partial(combine_kernel, n_ep, base, first, last, n_rows),
        in_specs=in_specs,
        out_specs=out_specs,
        out_shape=out_shape,
        scratch_shapes=[
            pltpu.VMEM((tok_dev * SUB, LANE), F32),
            pltpu.VMEM((SUB * pitch_for(cap), LANE), F32),
            pltpu.VMEM((2, cap, width), BF),
            pltpu.SMEM((2, 1, dg[0].shape[2]), F32),
            pltpu.SemaphoreType.DMA((2, 2)),
            pltpu.SemaphoreType.DMA,
        ],
        input_output_aliases={} if first or last else {4 + 2 * n_rows: 0},
        compiler_params=pltpu.CompilerParams(vmem_limit_bytes=VMEM_LIMIT),
        name="combine",
        cost_estimate=pl.CostEstimate(flops=n_rows * 3_000_000_000, bytes_accessed=n_rows * 3_000_000, transcendentals=0),
    )(*args)


def sort_assignments(ids_dev, gate_dev, n_exp, cap):
    n_assign = ids_dev.size
    key = ids_dev.reshape(-1) * n_assign + jnp.arange(n_assign, dtype=jnp.int32)
    key, gates = lax.sort((key, gate_dev.reshape(-1)), num_keys=1)
    edges = jnp.arange(n_exp + 1, dtype=jnp.int32) * n_assign
    starts = jnp.sum((key[None, :] < edges[:, None]).astype(jnp.int32), axis=1)
    counts = jnp.minimum(starts[1:] - starts[:-1], cap)
    pad = 2 * LANE
    asg = jnp.pad(key & (n_assign - 1), (0, pad))
    return asg, jnp.pad(gates, (0, pad)), starts[:-1], counts


def shared_backward(x_rows, g_rows, w_a, w_b, w_c):
    h_one = _dot(x_rows, w_a)
    h_three = _dot(x_rows, w_c)
    sig_one = jax.nn.sigmoid(h_one)
    silu_one = h_one * sig_one
    act_rows = (silu_one * h_three).astype(BF)
    d_act = _dot_t(g_rows, w_b)
    dh_one = (d_act * h_three * sig_one * (1.0 + h_one * (1.0 - sig_one))).astype(BF)
    dh_three = (d_act * silu_one).astype(BF)
    dx_rows = (_dot_t(dh_one, w_a) + _dot_t(dh_three, w_c)).astype(BF)
    return dx_rows, _dot_tn(x_rows, dh_one), _dot_tn(act_rows, g_rows), _dot_tn(x_rows, dh_three)


def solution(mesh):
    ep_size = mesh.shape["ep"]
    rows_size = mesh.shape["fsdp"]
    tok_spec = P(("fsdp", "ep"), None)
    in_specs = (tok_spec, tok_spec, tok_spec, tok_spec, P("ep", "fsdp", None), P("ep", None, "fsdp"), P("ep", "fsdp", None), P("fsdp", None), P(None, "fsdp"), P("fsdp", None))
    out_specs = (tok_spec, tok_spec, P("ep", "fsdp", None), P("ep", None, "fsdp"), P("ep", "fsdp", None), P("fsdp", None), P(None, "fsdp"), P("fsdp", None))
    cuts = (0, 4, 6, 7, 8)
    kernels = ["gather_0", "gather_1", "gather_2", "gather_3", "gather_4", "gather_5", "own_0", "own_1", "gather_6", "gather_7", "all_2", "other_0", "other_1"]
    kernels += ["all_3", "all_4", "all_5", "combine_0", "all_6", "combine_1", "all_7", "combine_2", "combine_3"]

    def swap_row(v):
        return lax.ppermute(v, "fsdp", [(i, rows_size - 1 - i) for i in range(rows_size)])

    def swap_ep(v, k):
        return lax.ppermute(v, "ep", [(i, i ^ k) for i in range(ep_size)])

    def device_step(x_loc, dy_loc, ids_loc, gate_loc, w_one, w_two, w_three, ws_one, ws_two, ws_three):
        tok_dev, top_k = ids_loc.shape
        assert top_k == SUB
        n_local = w_one.shape[0]
        n_exp = n_local * ep_size
        n_src = ep_size * rows_size
        n_col = x_loc.shape[1] // LANE
        cap = capacity_for(tok_dev, top_k, n_exp)
        n_grp = n_local // N_GROUP
        me, row = lax.axis_index("ep"), lax.axis_index("fsdp")
        place = jnp.stack([row, me]).astype(jnp.int32)

        near = (x_loc, dy_loc)
        far = tuple(swap_row(v) for v in near)
        near_x = tuple(swap_ep(v, 2) for v in near)
        near_c = tuple(swap_ep(v, 1) for v in near)

        w_mine = (w_one, w_three, jnp.swapaxes(w_two, 1, 2))
        w_far = []
        for g in range(N_GROUP):
            w_far.append(tuple(swap_row(w[g * n_grp:(g + 1) * n_grp]) for w in w_mine))

        ws_one_full = lax.all_gather(ws_one, "fsdp", axis=0, tiled=True)
        ws_three_full = lax.all_gather(ws_three, "fsdp", axis=0, tiled=True)
        ws_two_full = lax.all_gather(ws_two, "fsdp", axis=1, tiled=True)
        shared = shared_backward(x_loc, dy_loc, ws_one_full, ws_two_full, ws_three_full)
        dws_one = lax.psum(lax.psum_scatter(shared[1], "fsdp", scatter_dimension=0, tiled=True), "ep")
        dws_two = lax.psum(lax.psum_scatter(shared[2], "fsdp", scatter_dimension=1, tiled=True), "ep")
        dws_three = lax.psum(lax.psum_scatter(shared[3], "fsdp", scatter_dimension=0, tiled=True), "ep")

        ids_loc, gate_loc, shared = lax.optimization_barrier((ids_loc, gate_loc, shared))
        asg, gates, starts, counts = sort_assignments(ids_loc, gate_loc, n_exp, cap)
        n_list = asg.shape[0]
        meta = jnp.concatenate([(asg // top_k) * n_col, starts, counts])
        meta_all = lax.all_gather(meta, ("fsdp", "ep"), axis=0)
        gates_all = lax.all_gather(gates, ("fsdp", "ep"), axis=0)

        def gather(plane, bufs, x_src, dy_src):
            own = plane < ep_size
            if plane == 0:
                meta_s, gates_s = meta, gates
            else:
                src = jnp.bitwise_xor(me, plane % ep_size) + ep_size * (row if own else rows_size - 1 - row)
                meta_s = lax.dynamic_index_in_dim(meta_all, src, 0, keepdims=False)
                gates_s = lax.dynamic_index_in_dim(gates_all, src, 0, keepdims=False)
            starts_s = lax.dynamic_slice(meta_s, (n_list + me * n_local,), (n_local,))
            counts_s = lax.dynamic_slice(meta_s, (n_list + n_exp + me * n_local,), (n_local,))
            take = tuple(bufs) if own else tuple(bufs[:2])
            new = gather_call(plane, take, starts_s, counts_s, meta_s[:n_list], gates_s, x_src, dy_src, n_src, cap, own)
            return tuple(new) + tuple(bufs[len(new):])

        near_xc = tuple(swap_ep(v, 1) for v in near_x)
        far_x = tuple(swap_ep(v, 2) for v in far)
        far_c = tuple(swap_ep(v, 1) for v in far)
        far_xc = tuple(swap_ep(v, 1) for v in far_x)
        srcs = (near, near_c, near_x, near_xc, far, far_c, far_x, far_xc)
        bufs, grads = (), None
        back_rows, part_dg = [None] * N_GROUP, [None] * N_GROUP
        acc = None
        for name in kernels:
            kind, i = name.split("_")
            i = int(i)
            if kind == "gather":
                bufs = gather(i, bufs, *srcs[i])
                continue
            if kind == "combine":
                lo, hi = cuts[i], cuts[i + 1]
                dg = [part_dg[g][k] for k in range(ep_size) for g in range(lo, hi)]
                rows = [back_rows[g][k] for k in range(ep_size) for g in range(lo, hi)]
                final = shared[0] if hi == N_GROUP else None
                acc = combine_call(place, starts, counts, asg, dg, rows, lo * n_grp, acc, final, ep_size, tok_dev)
                continue
            xs, gs, ds = bufs
            out = expert_call(kind, place, xs, gs, ds, w_mine, w_far[i], i * n_grp, grads)
            if kind == "other":
                grads = out
                continue
            dx_g, dg_g, grads = out
            part_dg[i] = [dg_g[0]] + [swap_ep(dg_g[k], k) for k in range(1, ep_size)]
            back_rows[i] = [dx_g[0]] + [swap_ep(dx_g[k], k) for k in range(1, ep_size)]
        dx_loc, dg_tok = acc
        dw_one, dw_two, dw_three = grads
        return dx_loc, dg_tok[:, :top_k], dw_one, jnp.swapaxes(dw_two, 1, 2), dw_three, dws_one, dws_two, dws_three


    return jax.shard_map(device_step, mesh=mesh, in_specs=in_specs, out_specs=out_specs, check_vma=False)
```

time: 2710 us -> 2580 us (0.952)
  waiting for transfers between devices: 1280 us -> 1190 us
  other arithmetic: 71.7 us -> 23.4 us
  starting transfers between devices: 28.7 us -> 67.1 us
    ppermute x45 -> x60, waiting for transfers between devices: 1140 us -> 660 us  [swap_ep(): return lax.ppermute(v, 'ep', [(i, i ^ k) for i in range(ep_size)])]
    ppermute x2 -> x26, waiting for transfers between devices: 138 us -> 469 us  [swap_row(): lax.ppermute(v, 'fsdp', [(i, rows_size - 1 - i) for i in range(rows_size)])]
    pallas_call x8, Pallas kernels: 537 us -> 445 us  [gather_call(): pl.pallas_call(functools.partial(gather_kernel, own, cap, chunk), grid=(n...]
    psum x1, waiting for transfers between devices: 0.02 us -> 66 us  [device_step(): lax.psum(lax.psum_scatter(shared[1], 'fsdp', scatter_dimension=0, tiled=T...]
    pallas_call x3 -> x4, Pallas kernels: 241 us -> 288 us  [combine_call(): pl.pallas_call(functools.partial(combine_kernel, n_ep, base, first, last,...]
    concatenate x12 -> x1, other arithmetic: 47.3 us -> 0.01 us  [device_step(): meta = jnp.concatenate([asg // top_k * n_col, starts, counts])]
    pallas_call x8 -> x10, Pallas kernels: 370 us -> 405 us  [expert_call(): pl.pallas_call(functools.partial(expert_kernel, own, add, n_dst, cap, bas...]
  transfers between devices with their start and end apart: 61 -> 92, of which waited for: 27 -> 26; matrix products, arithmetic and copies ran while one was open for 5% -> 5% of each run, Pallas kernels for 41% -> 43%
where the time goes in v2:
time: 2580 us; the launch traced here: 2570 us
  waiting for transfers between devices  1190 us (46%)
  Pallas kernels  1140 us (44%)
  local copies, waits for them, and re-layouts  68.9 us (3%)
  starting transfers between devices  67.1 us (3%)
  matrix products  34.7 us (1%)
    ppermute x60, waiting for transfers between devices, swap_ep(): return lax.ppermute(v, 'ep', [(i, i ^ k) for i in range(ep_size)])  660 us
    ppermute x26, waiting for transfers between devices, swap_row(): lax.ppermute(v, 'fsdp', [(i, rows_size - 1 - i) for i in range(rows_size)])  469 us
    pallas_call x8, Pallas kernels, gather_call(): pl.pallas_call(functools.partial(gather_kernel, own, cap, chunk), grid=(n...  445 us
    pallas_call x10, Pallas kernels, expert_call(): pl.pallas_call(functools.partial(expert_kernel, own, add, n_dst, cap, bas...  405 us
    pallas_call x4, Pallas kernels, combine_call(): pl.pallas_call(functools.partial(combine_kernel, n_ep, base, first, last,...  288 us
    psum x1, waiting for transfers between devices, device_step(): lax.psum(lax.psum_scatter(shared[1], 'fsdp', scatter_dimension=0, tiled=T...  66 us
  transfers between devices with their start and end apart: 92, of which 26 were waited for; matrix products, arithmetic and copies ran while one was open for 5% of the time, Pallas kernels for 43%

profile of v2, /device:TPU:0, one launch (start us, length us, event | category | flops | bytes accessed | tf_op | source)
XLA Modules:
  0.0 2567.8 jit_solution(394600667176706990)
XLA Ops:
  132.3 58.7 %gather_own.4 = (bf16[64,8,160,896]{3,2,1,0:T(8,128)(2,1)}, bf16[64,8,160,896]{3,2,1,0:T(8,128)(2,1)}, bf16[64,4,160,896]{3,2,1,0:T(8,128)(2,1)}) custom-call(s32[64]{0:T(128)} %get-tuple-element.342.start_ref, s32[64]{0:T(128)} %get-tuple-element.341.cnt_ref, s32[33024]{0:T(1024)} %copy-done.14, f32[33024]{0:T(1024)} %copy-done.15, ...), custom_call_target="tpu_custom_call" | custom-call | flops 30000001024 | bytes 60000000 | tf_op jit(solution)/shard_map/gather_own/pallas_call | solution.py:112
  196.2 140.0 %collective-permute-done.10.d_hbm = bf16[4096,896]{1,0:T(8,128)(2,1)} collective-permute-done((bf16[4096,896]{1,0:T(8,128)(2,1)}, bf16[4096,896]{1,0:T(8,128)(2,1)}, u32[]{:S(2)}, u32[]{:S(2)}) %collective-permute-start.10) | collective-permute-done | bytes 7340064 | tf_op jit(solution)/shard_map/ppermute | solution.py:453
  347.6 58.4 %gather_own.5 = (bf16[64,8,160,896]{3,2,1,0:T(8,128)(2,1)}, bf16[64,8,160,896]{3,2,1,0:T(8,128)(2,1)}, bf16[64,4,160,896]{3,2,1,0:T(8,128)(2,1)}) custom-call(s32[64]{0:T(128)} %get-tuple-element.328.start_ref, s32[64]{0:T(128)} %get-tuple-element.327.cnt_ref, ...), custom_call_target="tpu_custom_call", output_to_operand_aliasing={{0}: (6, {}), {1}: (7, {}), {2}: (8, {})} | custom-call | flops 30000001024 | bytes 60000000 | tf_op jit(solution)/shard_map/gather_own/pallas_call | solution.py:112
  406.0 66.3 %collective-permute-done.34.rest_6_.rest_5_ = bf16[8,448,256]{2,1,0:T(8,128)(2,1)S(1)} collective-permute-done((bf16[8,448,256]{2,1,0:T(8,128)(2,1)S(1)}, bf16[8,448,256]{2,1,0:T(8,128)(2,1)S(1)}, u32[]{:S(2)}, u32[]{:S(2)}) %collective-permute-start.34) | collective-permute-done | bytes 1835040 | tf_op jit(solution)/shard_map/ppermute | solution.py:450
  474.4 58.3 %gather_own.6 = (bf16[64,8,160,896]{3,2,1,0:T(8,128)(2,1)}, bf16[64,8,160,896]{3,2,1,0:T(8,128)(2,1)}, bf16[64,4,160,896]{3,2,1,0:T(8,128)(2,1)}) custom-call(s32[64]{0:T(128)} %get-tuple-element.330.start_ref, s32[64]{0:T(128)} %get-tuple-element.329.cnt_ref, ...), custom_call_target="tpu_custom_call", output_to_operand_aliasing={{0}: (6, {}), {1}: (7, {}), {2}: (8, {})} | custom-call | flops 30000001024 | bytes 60000000 | tf_op jit(solution)/shard_map/gather_own/pallas_call | solution.py:112
  533.7 58.5 %gather_own.7 = (bf16[64,8,160,896]{3,2,1,0:T(8,128)(2,1)}, bf16[64,8,160,896]{3,2,1,0:T(8,128)(2,1)}, bf16[64,4,160,896]{3,2,1,0:T(8,128)(2,1)}) custom-call(s32[64]{0:T(128)} %get-tuple-element.332.start_ref, s32[64]{0:T(128)} %get-tuple-element.331.cnt_ref, ...), custom_call_target="tpu_custom_call", output_to_operand_aliasing={{0}: (6, {}), {1}: (7, {}), {2}: (8, {})} | custom-call | flops 30000001024 | bytes 60000000 | tf_op jit(solution)/shard_map/gather_own/pallas_call | solution.py:112
  593.4 53.0 %gather_other.4 = (bf16[64,8,160,896]{3,2,1,0:T(8,128)(2,1)}, bf16[64,8,160,896]{3,2,1,0:T(8,128)(2,1)}) custom-call(s32[64]{0:T(128)} %get-tuple-element.334.start_ref, s32[64]{0:T(128)} %get-tuple-element.333.cnt_ref, s32[33024]{0:T(1024)} %slice_reduce_fusion.3.tok_ref, ...), custom_call_target="tpu_custom_call", output_to_operand_aliasing={{0}: (6, {}), {1}: (7, {})} | custom-call | flops 30000001024 | bytes 60000000 | tf_op jit(solution)/shard_map/gather_other/pallas_call | solution.py:112
  649.3 140.3 %collective-permute-done.4.d_hbm = bf16[4096,896]{1,0:T(8,128)(2,1)} collective-permute-done((bf16[4096,896]{1,0:T(8,128)(2,1)}, bf16[4096,896]{1,0:T(8,128)(2,1)}, u32[]{:S(2)}, u32[]{:S(2)}) %collective-permute-start.4) | collective-permute-done | bytes 7340064 | tf_op jit(solution)/shard_map/ppermute | solution.py:453
  789.6 52.6 %gather_other.5 = (bf16[64,8,160,896]{3,2,1,0:T(8,128)(2,1)}, bf16[64,8,160,896]{3,2,1,0:T(8,128)(2,1)}) custom-call(s32[64]{0:T(128)} %get-tuple-element.336.start_ref, s32[64]{0:T(128)} %get-tuple-element.335.cnt_ref, s32[33024]{0:T(1024)} %slice_reduce_fusion.4.tok_ref, ...), custom_call_target="tpu_custom_call", output_to_operand_aliasing={{0}: (6, {}), {1}: (7, {})} | custom-call | flops 30000001024 | bytes 60000000 | tf_op jit(solution)/shard_map/gather_other/pallas_call | solution.py:112
  908.4 52.7 %gather_other.6 = (bf16[64,8,160,896]{3,2,1,0:T(8,128)(2,1)}, bf16[64,8,160,896]{3,2,1,0:T(8,128)(2,1)}) custom-call(s32[64]{0:T(128)} %get-tuple-element.338.start_ref, s32[64]{0:T(128)} %get-tuple-element.337.cnt_ref, s32[33024]{0:T(1024)} %slice_reduce_fusion.5.tok_ref, ...), custom_call_target="tpu_custom_call", output_to_operand_aliasing={{0}: (6, {}), {1}: (7, {})} | custom-call | flops 30000001024 | bytes 60000000 | tf_op jit(solution)/shard_map/gather_other/pallas_call | solution.py:112
  964.5 52.7 %gather_other.7 = (bf16[64,8,160,896]{3,2,1,0:T(8,128)(2,1)}, bf16[64,8,160,896]{3,2,1,0:T(8,128)(2,1)}) custom-call(s32[64]{0:T(128)} %get-tuple-element.340.start_ref, s32[64]{0:T(128)} %get-tuple-element.339.cnt_ref, s32[33024]{0:T(1024)} %slice_reduce_fusion.6.tok_ref, ...), custom_call_target="tpu_custom_call", output_to_operand_aliasing={{0}: (6, {}), {1}: (7, {})} | custom-call | flops 30000001024 | bytes 60000000 | tf_op jit(solution)/shard_map/gather_other/pallas_call | solution.py:112
  1075.1 38.5 %collective-permute-done.27.rest_5_ = bf16[8,448,256]{2,1,0:T(8,128)(2,1)} collective-permute-done((bf16[8,448,256]{2,1,0:T(8,128)(2,1)}, bf16[8,448,256]{2,1,0:T(8,128)(2,1)}, u32[]{:S(2)}, u32[]{:S(2)}) %collective-permute-start.27) | collective-permute-done | bytes 1835040 | tf_op jit(solution)/shard_map/ppermute | solution.py:450
  1114.5 48.2 %shard_map.163 = (bf16[8,160,896]{2,1,0:T(8,128)(2,1)}, bf16[8,160,896]{2,1,0:T(8,128)(2,1)}, bf16[8,160,896]{2,1,0:T(8,128)(2,1)}, bf16[8,160,896]{2,1,0:T(8,12...) custom-call(s32[2]{0:T(128)} %pad_add_fusion.1.place_ref.refs_0_, ...), custom_call_target="tpu_custom_call", output_to_operand_aliasing={{8}: (10, {}), {9}: (11, {}), {10}: (12, {})} | custom-call | flops 28185722880 | bytes 72000000 | tf_op jit(solution)/shard_map/pallas_call | solution.py:263
  1428.1 39.3 %collective-permute-done.18.rest_5_ = bf16[8,448,256]{2,1,0:T(8,128)(2,1)} collective-permute-done((bf16[8,448,256]{2,1,0:T(8,128)(2,1)}, bf16[8,448,256]{2,1,0:T(8,128)(2,1)}, u32[]{:S(2)}, u32[]{:S(2)}) %collective-permute-start.18) | collective-permute-done | bytes 1835040 | tf_op jit(solution)/shard_map/ppermute | solution.py:450
  1506.9 48.2 %shard_map.166 = (bf16[8,160,896]{2,1,0:T(8,128)(2,1)}, bf16[8,160,896]{2,1,0:T(8,128)(2,1)}, bf16[8,160,896]{2,1,0:T(8,128)(2,1)}, bf16[8,160,896]{2,1,0:T(8,12...) custom-call(s32[2]{0:T(128)} %pad_add_fusion.1.place_ref.refs_0_, ...), custom_call_target="tpu_custom_call", output_to_operand_aliasing={{8}: (10, {}), {9}: (11, {}), {10}: (12, {})} | custom-call | flops 28185722880 | bytes 72000000 | tf_op jit(solution)/shard_map/pallas_call | solution.py:263
  1588.2 48.2 %shard_map.167 = (bf16[8,160,896]{2,1,0:T(8,128)(2,1)}, bf16[8,160,896]{2,1,0:T(8,128)(2,1)}, bf16[8,160,896]{2,1,0:T(8,128)(2,1)}, bf16[8,160,896]{2,1,0:T(8,12...) custom-call(s32[2]{0:T(128)} %pad_add_fusion.1.place_ref.refs_0_, ...), custom_call_target="tpu_custom_call", output_to_operand_aliasing={{8}: (10, {}), {9}: (11, {}), {10}: (12, {})} | custom-call | flops 28185722880 | bytes 72000000 | tf_op jit(solution)/shard_map/pallas_call | solution.py:263
  1639.3 48.5 %shard_map.168 = (bf16[8,160,896]{2,1,0:T(8,128)(2,1)}, bf16[8,160,896]{2,1,0:T(8,128)(2,1)}, bf16[8,160,896]{2,1,0:T(8,128)(2,1)}, bf16[8,160,896]{2,1,0:T(8,12...) custom-call(s32[2]{0:T(128)} %pad_add_fusion.1.place_ref.refs_0_, ...), custom_call_target="tpu_custom_call", output_to_operand_aliasing={{8}: (10, {}), {9}: (11, {}), {10}: (12, {})} | custom-call | flops 28185722880 | bytes 72000000 | tf_op jit(solution)/shard_map/pallas_call | solution.py:263
  1690.5 48.1 %collective-permute-done.66.refs_12_ = bf16[8,160,896]{2,1,0:T(8,128)(2,1)} collective-permute-done((bf16[8,160,896]{2,1,0:T(8,128)(2,1)}, bf16[8,160,896]{2,1,0:T(8,128)(2,1)}, u32[]{:S(2)}, u32[]{:S(2)}) %collective-permute-start.66) | collective-permute-done | bytes 2293792 | tf_op jit(solution)/shard_map/ppermute | solution.py:453
  1738.6 48.1 %collective-permute-done.70.refs_16_ = bf16[8,160,896]{2,1,0:T(8,128)(2,1)} collective-permute-done((bf16[8,160,896]{2,1,0:T(8,128)(2,1)}, bf16[8,160,896]{2,1,0:T(8,128)(2,1)}, u32[]{:S(2)}, u32[]{:S(2)}) %collective-permute-start.70) | collective-permute-done | bytes 2293792 | tf_op jit(solution)/shard_map/ppermute | solution.py:453
  1788.6 48.2 %shard_map.169 = (bf16[8,160,896]{2,1,0:T(8,128)(2,1)}, bf16[8,160,896]{2,1,0:T(8,128)(2,1)}, bf16[8,160,896]{2,1,0:T(8,128)(2,1)}, bf16[8,160,896]{2,1,0:T(8,12...) custom-call(s32[2]{0:T(128)} %pad_add_fusion.1.place_ref.refs_0_, ...), custom_call_target="tpu_custom_call", output_to_operand_aliasing={{8}: (10, {}), {9}: (11, {}), {10}: (12, {})} | custom-call | flops 28185722880 | bytes 72000000 | tf_op jit(solution)/shard_map/pallas_call | solution.py:263
  1840.1 48.5 %shard_map.170 = (bf16[8,160,896]{2,1,0:T(8,128)(2,1)}, bf16[8,160,896]{2,1,0:T(8,128)(2,1)}, bf16[8,160,896]{2,1,0:T(8,128)(2,1)}, bf16[8,160,896]{2,1,0:T(8,12...) custom-call(s32[2]{0:T(128)} %pad_add_fusion.1.place_ref.refs_0_, ...), custom_call_target="tpu_custom_call", output_to_operand_aliasing={{8}: (10, {}), {9}: (11, {}), {10}: (12, {})} | custom-call | flops 28185722880 | bytes 72000000 | tf_op jit(solution)/shard_map/pallas_call | solution.py:263
  1899.5 46.1 %collective-permute-done.69.refs_15_ = bf16[8,160,896]{2,1,0:T(8,128)(2,1)} collective-permute-done((bf16[8,160,896]{2,1,0:T(8,128)(2,1)}, bf16[8,160,896]{2,1,0:T(8,128)(2,1)}, u32[]{:S(2)}, u32[]{:S(2)}) %collective-permute-start.69) | collective-permute-done | bytes 2293792 | tf_op jit(solution)/shard_map/ppermute | solution.py:453
  1945.6 48.1 %collective-permute-done.73.refs_19_ = bf16[8,160,896]{2,1,0:T(8,128)(2,1)} collective-permute-done((bf16[8,160,896]{2,1,0:T(8,128)(2,1)}, bf16[8,160,896]{2,1,0:T(8,128)(2,1)}, u32[]{:S(2)}, u32[]{:S(2)}) %collective-permute-start.73) | collective-permute-done | bytes 2293792 | tf_op jit(solution)/shard_map/ppermute | solution.py:453
  1995.9 48.0 %collective-permute-done.68.refs_14_ = bf16[8,160,896]{2,1,0:T(8,128)(2,1)} collective-permute-done((bf16[8,160,896]{2,1,0:T(8,128)(2,1)}, bf16[8,160,896]{2,1,0:T(8,128)(2,1)}, u32[]{:S(2)}, u32[]{:S(2)}) %collective-permute-start.68) | collective-permute-done | bytes 2293792 | tf_op jit(solution)/shard_map/ppermute | solution.py:453
  2050.0 66.0 %all-reduce.5.cloned.1.call-done = (f32[448,256]{0,1:T(8,128)}, f32[256,448]{1,0:T(8,128)}, f32[448,256]{0,1:T(8,128)}) async-done(((f32[448,256]{0,1:T(8,128)}, f32[256,448]{1,0:T(8,128)}, f32[448,256]{0,1:T(8,128)}), (f32[448,256]{0,1:T(8,128)}, f32[256,448]{1,0:T(8,128)}, f32[448,256]{0,1:T(8,128)})) %all-reduce.5.cloned.1.call-update) | async-done | bytes 1376272 | tf_op jit(solution)/shard_map/psum | solution.py:481
  2122.1 45.4 %collective-permute-done.53.refs_9_ = bf16[8,160,896]{2,1,0:T(8,128)(2,1)} collective-permute-done((bf16[8,160,896]{2,1,0:T(8,128)(2,1)}, bf16[8,160,896]{2,1,0:T(8,128)(2,1)}, u32[]{:S(2)}, u32[]{:S(2)}) %collective-permute-start.53) | collective-permute-done | bytes 2293792 | tf_op jit(solution)/shard_map/ppermute | solution.py:453
  2167.5 48.1 %collective-permute-done.55.refs_11_ = bf16[8,160,896]{2,1,0:T(8,128)(2,1)} collective-permute-done((bf16[8,160,896]{2,1,0:T(8,128)(2,1)}, bf16[8,160,896]{2,1,0:T(8,128)(2,1)}, u32[]{:S(2)}, u32[]{:S(2)}) %collective-permute-start.55) | collective-permute-done | bytes 2293792 | tf_op jit(solution)/shard_map/ppermute | solution.py:453
  2217.8 128.6 %combine.4.refs_20_ = f32[32768,128]{1,0:T(8,128)} custom-call(s32[2]{0:T(128)} %pad_add_fusion.1.place_ref.refs_0_, s32[256]{0:T(256)} %copy-done.22, s32[256]{0:T(256)} %copy-done.21, s32[33024]{0:T(1024)} %get-tuple-element.344.refs_3_, bf16[8,160,896]{2,1,0:T(8,128)(2,1)} %get-tuple-element.214.refs_4_, bf16[8,160,896]{2,1,0:T(8,128)(2,1)} %get-tuple-element.215.refs_5_, ...), custom_call_target="tpu_custom_call" | custom-call | flops 48000000000 | bytes 48000000 | tf_op jit(solution)/shard_map/combine/pallas_call | solution.py:394
  2348.3 71.8 %combine.5.refs_12_ = f32[32768,128]{1,0:T(8,128)} custom-call(s32[2]{0:T(128)} %pad_add_fusion.1.place_ref.refs_0_, s32[256]{0:T(256)} %copy-done.22, s32[256]{0:T(256)} %copy-done.21, s32[33024]{0:T(1024)} %get-tuple-element.344.refs_3_, bf16[8,160,896]{2,1,0:T(8,128)(2,1)} %get-tuple-element.198.refs_4_, ...), custom_call_target="tpu_custom_call", output_to_operand_aliasing={{}: (20, {})} | custom-call | flops 24000000000 | bytes 24000000 | tf_op jit(solution)/shard_map/combine/pallas_call | solution.py:394
  2422.4 42.8 %combine.6.refs_12_ = f32[32768,128]{1,0:T(8,128)} custom-call(s32[2]{0:T(128)} %pad_add_fusion.1.place_ref.refs_0_, s32[256]{0:T(256)} %copy-done.22, s32[256]{0:T(256)} %copy-done.21, s32[33024]{0:T(1024)} %get-tuple-element.344.refs_3_, bf16[8,160,896]{2,1,0:T(8,128)(2,1)} %get-tuple-element.190.refs_4_, ...), custom_call_target="tpu_custom_call", output_to_operand_aliasing={{}: (12, {})} | custom-call | flops 12000000000 | bytes 12000000 | tf_op jit(solution)/shard_map/combine/pallas_call | solution.py:394
  2465.2 46.0 %collective-permute-done.42.refs_10_ = f32[8,1,256]{2,1,0:T(1,128)S(1)} collective-permute-done((f32[8,1,256]{2,1,0:T(1,128)S(1)}, f32[8,1,256]{2,1,0:T(1,128)S(1)}, u32[]{:S(2)}, u32[]{:S(2)}) %collective-permute-start.42) | collective-permute-done | bytes 8224 | tf_op jit(solution)/shard_map/ppermute | solution.py:453
  2511.8 45.3 %combine.7 = (bf16[4096,896]{1,0:T(8,128)(2,1)}, f32[4096,128]{1,0:T(8,128)}) custom-call(s32[2]{0:T(128)} %pad_add_fusion.1.place_ref.refs_0_, s32[256]{0:T(256)} %copy-done.22, s32[256]{0:T(256)} %copy-done.21, s32[33024]{0:T(1024)} %get-tuple-element.344.refs_3_, bf16[8,160,896]{2,1,0:T(8,128)(2,1)} %get-tuple-element.182.refs_4_, ...), custom_call_target="tpu_custom_call" | custom-call | flops 12000000000 | bytes 12000000 | tf_op jit(solution)/shard_map/combine/pallas_call | solution.py:394
  (404 shorter events, 659.0 us)
Async XLA Ops:
  8.9 327.3 %collective-permute-start.8 = (bf16[4096,896]{1,0:T(8,128)(2,1)}, bf16[4096,896]{1,0:T(8,128)(2,1)}, u32[]{:S(2)}, u32[]{:S(2)}) collective-permute-start(bf16[4096,896]{1,0:T(8,128)(2,1)} %x_hbm.1), channel_id=1, source_target_pairs={{0,2},{1,3},{2,0},{3,1},{4,6},{5,7},{6,4},{7,5}} | collective-permute-start | bytes 22020104 | tf_op jit(solution)/shard_map/ppermute | solution.py:453
  11.4 324.8 %collective-permute-start.10 = (bf16[4096,896]{1,0:T(8,128)(2,1)}, bf16[4096,896]{1,0:T(8,128)(2,1)}, u32[]{:S(2)}, u32[]{:S(2)}) collective-permute-start(bf16[4096,896]{1,0:T(8,128)(2,1)} %d_hbm.1), channel_id=1, source_target_pairs={{0,2},{1,3},{2,0},{3,1},{4,6},{5,7},{6,4},{7,5}} | collective-permute-start | bytes 22020104 | tf_op jit(solution)/shard_map/ppermute | solution.py:453
  91.8 244.9 %all-gather.7.cloned.1.call-start = ((), (), s32[]{:S(2)}) async-start(), calls=%async_computation.3 | async-start | bytes 1207296 | tf_op jit(solution)/shard_map/all_gather | solution.py:489
  97.6 1946.3 %reduce-scatter.12.cloned.1.call-start = ((), (), s32[]{:S(2)}) async-start(), calls=%async_computation.6 | async-start | bytes 1376256
  97.7 248.2 %collective-permute-start.13 = (bf16[4096,896]{1,0:T(8,128)(2,1)}, bf16[4096,896]{1,0:T(8,128)(2,1)}, u32[]{:S(2)}, u32[]{:S(2)}) collective-permute-start(bf16[4096,896]{1,0:T(8,128)(2,1)} %d_hbm.1), channel_id=1, source_target_pairs={{0,1},{1,0},{2,3},{3,2},{4,5},{5,4},{6,7},{7,6}} | collective-permute-start | bytes 22020104 | tf_op jit(solution)/shard_map/ppermute | solution.py:453
  97.7 249.9 %collective-permute-start = (bf16[4096,896]{1,0:T(8,128)(2,1)}, bf16[4096,896]{1,0:T(8,128)(2,1)}, u32[]{:S(2)}, u32[]{:S(2)}) collective-permute-start(bf16[4096,896]{1,0:T(8,128)(2,1)} %x_hbm.1), channel_id=1, source_target_pairs={{0,4},{4,0},{1,5},{5,1},{2,6},{6,2},{3,7},{7,3}} | collective-permute-start | bytes 22020104 | tf_op jit(solution)/shard_map/ppermute | solution.py:450
  100.3 1945.7 %reduce-scatter.10.cloned.1.call-start = ((), (), s32[]{:S(2)}) async-start(), calls=%async_computation.5 | async-start | bytes 1376256
  195.6 278.2 %collective-permute-start.3 = (bf16[4096,896]{1,0:T(8,128)(2,1)}, bf16[4096,896]{1,0:T(8,128)(2,1)}, u32[]{:S(2)}, u32[]{:S(2)}) collective-permute-start(bf16[4096,896]{1,0:T(8,128)(2,1)} %d_hbm.1), channel_id=1, source_target_pairs={{0,4},{4,0},{1,5},{5,1},{2,6},{6,2},{3,7},{7,3}} | collective-permute-start | bytes 22020104 | tf_op jit(solution)/shard_map/ppermute | solution.py:450
  336.2 196.5 %collective-permute-start.9 = (bf16[4096,896]{1,0:T(8,128)(2,1)}, bf16[4096,896]{1,0:T(8,128)(2,1)}, u32[]{:S(2)}, u32[]{:S(2)}) collective-permute-start(bf16[4096,896]{1,0:T(8,128)(2,1)} %collective-permute-done.8.x_hbm), channel_id=1, source_target_pairs={{0,1},{1,0},{2,3},{3,2},{4,5},{5,4},{6,7},{7,6}} | collective-permute-start | bytes 22020104 | tf_op jit(solution)/shard_map/ppermute | solution.py:453
  347.6 299.7 %collective-permute-start.6 = (bf16[4096,896]{1,0:T(8,128)(2,1)}, bf16[4096,896]{1,0:T(8,128)(2,1)}, u32[]{:S(2)}, u32[]{:S(2)}) collective-permute-start(bf16[4096,896]{1,0:T(8,128)(2,1)} %collective-permute-done.x_hbm), channel_id=1, source_target_pairs={{0,1},{1,0},{2,3},{3,2},{4,5},{5,4},{6,7},{7,6}} | collective-permute-start | bytes 22020104 | tf_op jit(solution)/shard_map/ppermute | solution.py:453
  473.8 315.9 %collective-permute-start.4 = (bf16[4096,896]{1,0:T(8,128)(2,1)}, bf16[4096,896]{1,0:T(8,128)(2,1)}, u32[]{:S(2)}, u32[]{:S(2)}) collective-permute-start(bf16[4096,896]{1,0:T(8,128)(2,1)} %collective-permute-done.3.d_hbm), channel_id=1, source_target_pairs={{0,2},{1,3},{2,0},{3,1},{4,6},{5,7},{6,4},{7,5}} | collective-permute-start | bytes 22020104 | tf_op jit(solution)/shard_map/ppermute | solution.py:453
  646.4 227.3 %collective-permute-start.31 = (bf16[8,448,256]{2,1,0:T(8,128)(2,1)}, bf16[8,448,256]{2,1,0:T(8,128)(2,1)}, u32[]{:S(2)}, u32[]{:S(2)}) collective-permute-start(bf16[8,448,256]{2,1,0:T(8,128)(2,1)} %get-tuple-element.296), channel_id=1, source_target_pairs={{0,4},{4,0},{1,5},{5,1},{2,6},{6,2},{3,7},{7,3}} | collective-permute-start | bytes 5505032 | tf_op jit(solution)/shard_map/ppermute | solution.py:450
  647.3 227.4 %collective-permute-start.29 = (bf16[8,448,256]{2,1,0:T(8,128)(2,1)}, bf16[8,448,256]{2,1,0:T(8,128)(2,1)}, u32[]{:S(2)}, u32[]{:S(2)}) collective-permute-start(bf16[8,448,256]{2,1,0:T(8,128)(2,1)} %get-tuple-element.312), channel_id=1, source_target_pairs={{0,4},{4,0},{1,5},{5,1},{2,6},{6,2},{3,7},{7,3}} | collective-permute-start | bytes 5505032 | tf_op jit(solution)/shard_map/ppermute | solution.py:450
  648.5 227.3 %collective-permute-start.30 = (bf16[8,448,256]{2,1,0:T(8,128)(2,1)}, bf16[8,448,256]{2,1,0:T(8,128)(2,1)}, u32[]{:S(2)}, u32[]{:S(2)}) collective-permute-start(bf16[8,448,256]{2,1,0:T(8,128)(2,1)} %get-tuple-element.304), channel_id=1, source_target_pairs={{0,4},{4,0},{1,5},{5,1},{2,6},{6,2},{3,7},{7,3}} | collective-permute-start | bytes 5505032 | tf_op jit(solution)/shard_map/ppermute | solution.py:450
  649.3 313.1 %collective-permute-start.2 = (bf16[4096,896]{1,0:T(8,128)(2,1)}, bf16[4096,896]{1,0:T(8,128)(2,1)}, u32[]{:S(2)}, u32[]{:S(2)}) collective-permute-start(bf16[4096,896]{1,0:T(8,128)(2,1)} %collective-permute-done.1.x_hbm), channel_id=1, source_target_pairs={{0,1},{1,0},{2,3},{3,2},{4,5},{5,4},{6,7},{7,6}} | collective-permute-start | bytes 22020104 | tf_op jit(solution)/shard_map/ppermute | solution.py:453
  1034.8 196.7 %collective-permute-start.24 = (bf16[8,448,256]{2,1,0:T(8,128)(2,1)}, bf16[8,448,256]{2,1,0:T(8,128)(2,1)}, u32[]{:S(2)}, u32[]{:S(2)}) collective-permute-start(bf16[8,448,256]{2,1,0:T(8,128)(2,1)} %get-tuple-element.306), channel_id=1, source_target_pairs={{0,4},{4,0},{1,5},{5,1},{2,6},{6,2},{3,7},{7,3}} | collective-permute-start | bytes 5505032 | tf_op jit(solution)/shard_map/ppermute | solution.py:450
  1074.1 196.6 %collective-permute-start.22 = (bf16[8,448,256]{2,1,0:T(8,128)(2,1)}, bf16[8,448,256]{2,1,0:T(8,128)(2,1)S(1)}, u32[]{:S(2)}, u32[]{:S(2)}) collective-permute-start(bf16[8,448,256]{2,1,0:T(8,128)(2,1)} %get-tuple-element.299), channel_id=1, source_target_pairs={{0,4},{4,0},{1,5},{5,1},{2,6},{6,2},{3,7},{7,3}} | collective-permute-start | bytes 5505032 | tf_op jit(solution)/shard_map/ppermute | solution.py:450
  1113.5 196.5 %collective-permute-start.20 = (bf16[8,448,256]{2,1,0:T(8,128)(2,1)}, bf16[8,448,256]{2,1,0:T(8,128)(2,1)S(1)}, u32[]{:S(2)}, u32[]{:S(2)}) collective-permute-start(bf16[8,448,256]{2,1,0:T(8,128)(2,1)} %get-tuple-element.315), channel_id=1, source_target_pairs={{0,4},{4,0},{1,5},{5,1},{2,6},{6,2},{3,7},{7,3}} | collective-permute-start | bytes 5505032 | tf_op jit(solution)/shard_map/ppermute | solution.py:450
  1162.7 200.3 %collective-permute-start.21 = (bf16[8,448,256]{2,1,0:T(8,128)(2,1)}, bf16[8,448,256]{2,1,0:T(8,128)(2,1)}, u32[]{:S(2)}, u32[]{:S(2)}) collective-permute-start(bf16[8,448,256]{2,1,0:T(8,128)(2,1)} %get-tuple-element.307), channel_id=1, source_target_pairs={{0,4},{4,0},{1,5},{5,1},{2,6},{6,2},{3,7},{7,3}} | collective-permute-start | bytes 5505032 | tf_op jit(solution)/shard_map/ppermute | solution.py:450
  1192.2 196.6 %collective-permute-start.19 = (bf16[8,448,256]{2,1,0:T(8,128)(2,1)}, bf16[8,448,256]{2,1,0:T(8,128)(2,1)}, u32[]{:S(2)}, u32[]{:S(2)}) collective-permute-start(bf16[8,448,256]{2,1,0:T(8,128)(2,1)} %get-tuple-element.300), channel_id=1, source_target_pairs={{0,4},{4,0},{1,5},{5,1},{2,6},{6,2},{3,7},{7,3}} | collective-permute-start | bytes 5505032 | tf_op jit(solution)/shard_map/ppermute | solution.py:450
  1231.5 196.6 %collective-permute-start.17 = (bf16[8,448,256]{2,1,0:T(8,128)(2,1)}, bf16[8,448,256]{2,1,0:T(8,128)(2,1)}, u32[]{:S(2)}, u32[]{:S(2)}) collective-permute-start(bf16[8,448,256]{2,1,0:T(8,128)(2,1)} %get-tuple-element.316), channel_id=1, source_target_pairs={{0,4},{4,0},{1,5},{5,1},{2,6},{6,2},{3,7},{7,3}} | collective-permute-start | bytes 5505032 | tf_op jit(solution)/shard_map/ppermute | solution.py:450
  1270.7 196.7 %collective-permute-start.18 = (bf16[8,448,256]{2,1,0:T(8,128)(2,1)}, bf16[8,448,256]{2,1,0:T(8,128)(2,1)}, u32[]{:S(2)}, u32[]{:S(2)}) collective-permute-start(bf16[8,448,256]{2,1,0:T(8,128)(2,1)} %get-tuple-element.308), channel_id=1, source_target_pairs={{0,4},{4,0},{1,5},{5,1},{2,6},{6,2},{3,7},{7,3}} | collective-permute-start | bytes 5505032 | tf_op jit(solution)/shard_map/ppermute | solution.py:450
  1310.1 196.7 %collective-permute-start.16 = (bf16[8,448,256]{2,1,0:T(8,128)(2,1)}, bf16[8,448,256]{2,1,0:T(8,128)(2,1)}, u32[]{:S(2)}, u32[]{:S(2)}) collective-permute-start(bf16[8,448,256]{2,1,0:T(8,128)(2,1)} %get-tuple-element.301), channel_id=1, source_target_pairs={{0,4},{4,0},{1,5},{5,1},{2,6},{6,2},{3,7},{7,3}} | collective-permute-start | bytes 5505032 | tf_op jit(solution)/shard_map/ppermute | solution.py:450
  1363.1 192.0 %collective-permute-start.14 = (bf16[8,448,256]{2,1,0:T(8,128)(2,1)}, bf16[8,448,256]{2,1,0:T(8,128)(2,1)S(1)}, u32[]{:S(2)}, u32[]{:S(2)}) collective-permute-start(bf16[8,448,256]{2,1,0:T(8,128)(2,1)} %get-tuple-element.317), channel_id=1, source_target_pairs={{0,4},{4,0},{1,5},{5,1},{2,6},{6,2},{3,7},{7,3}} | collective-permute-start | bytes 5505032 | tf_op jit(solution)/shard_map/ppermute | solution.py:450
  1388.8 195.9 %collective-permute-start.15 = (bf16[8,448,256]{2,1,0:T(8,128)(2,1)}, bf16[8,448,256]{2,1,0:T(8,128)(2,1)S(1)}, u32[]{:S(2)}, u32[]{:S(2)}) collective-permute-start(bf16[8,448,256]{2,1,0:T(8,128)(2,1)} %get-tuple-element.309), channel_id=1, source_target_pairs={{0,4},{4,0},{1,5},{5,1},{2,6},{6,2},{3,7},{7,3}} | collective-permute-start | bytes 5505032 | tf_op jit(solution)/shard_map/ppermute | solution.py:450
  1898.9 217.1 %all-reduce.5.cloned.1.call-start = ((), (), s32[]{:S(2)}) async-start(), calls=%async_computation.8 | async-start | bytes 3145728 | tf_op jit(solution)/shard_map/psum | solution.py:481
  1899.5 221.6 %collective-permute-start.72 = (bf16[8,160,896]{2,1,0:T(8,128)(2,1)S(1)}, bf16[8,160,896]{2,1,0:T(8,128)(2,1)}, u32[]{:S(2)}, u32[]{:S(2)}) collective-permute-start(bf16[8,160,896]{2,1,0:T(8,128)(2,1)S(1)} %copy-done.23), channel_id=1, source_target_pairs={{0,3},{1,2},{2,1},{3,0},{4,7},{5,6},{6,5},{7,4}} | collective-permute-start | bytes 6881288 | tf_op jit(solution)/shard_map/ppermute | solution.py:453
  1994.5 221.1 %collective-permute-start.55 = (bf16[8,160,896]{2,1,0:T(8,128)(2,1)}, bf16[8,160,896]{2,1,0:T(8,128)(2,1)}, u32[]{:S(2)}, u32[]{:S(2)}) collective-permute-start(bf16[8,160,896]{2,1,0:T(8,128)(2,1)} %get-tuple-element.205), channel_id=1, source_target_pairs={{0,3},{1,2},{2,1},{3,0},{4,7},{5,6},{6,5},{7,4}} | collective-permute-start | bytes 6881288 | tf_op jit(solution)/shard_map/ppermute | solution.py:453
  2121.0 225.4 %collective-permute-start.52 = (bf16[8,160,896]{2,1,0:T(8,128)(2,1)}, bf16[8,160,896]{2,1,0:T(8,128)(2,1)}, u32[]{:S(2)}, u32[]{:S(2)}) collective-permute-start(bf16[8,160,896]{2,1,0:T(8,128)(2,1)} %get-tuple-element.202), channel_id=1, source_target_pairs={{0,2},{1,3},{2,0},{3,1},{4,6},{5,7},{6,4},{7,5}} | collective-permute-start | bytes 6881288 | tf_op jit(solution)/shard_map/ppermute | solution.py:453
  2121.3 225.2 %collective-permute-start.54 = (bf16[8,160,896]{2,1,0:T(8,128)(2,1)}, bf16[8,160,896]{2,1,0:T(8,128)(2,1)}, u32[]{:S(2)}, u32[]{:S(2)}) collective-permute-start(bf16[8,160,896]{2,1,0:T(8,128)(2,1)} %get-tuple-element.204), channel_id=1, source_target_pairs={{0,3},{1,2},{2,1},{3,0},{4,7},{5,6},{6,5},{7,4}} | collective-permute-start | bytes 6881288 | tf_op jit(solution)/shard_map/ppermute | solution.py:453
  2215.6 204.5 %collective-permute-start.45 = (bf16[8,160,896]{2,1,0:T(8,128)(2,1)}, bf16[8,160,896]{2,1,0:T(8,128)(2,1)}, u32[]{:S(2)}, u32[]{:S(2)}) collective-permute-start(bf16[8,160,896]{2,1,0:T(8,128)(2,1)} %get-tuple-element.192), channel_id=1, source_target_pairs={{0,2},{1,3},{2,0},{3,1},{4,6},{5,7},{6,4},{7,5}} | collective-permute-start | bytes 6881288 | tf_op jit(solution)/shard_map/ppermute | solution.py:453
  2216.4 204.9 %collective-permute-start.46 = (bf16[8,160,896]{2,1,0:T(8,128)(2,1)}, bf16[8,160,896]{2,1,0:T(8,128)(2,1)}, u32[]{:S(2)}, u32[]{:S(2)}) collective-permute-start(bf16[8,160,896]{2,1,0:T(8,128)(2,1)} %get-tuple-element.193), channel_id=1, source_target_pairs={{0,3},{1,2},{2,1},{3,0},{4,7},{5,6},{6,5},{7,4}} | collective-permute-start | bytes 6881288 | tf_op jit(solution)/shard_map/ppermute | solution.py:453
  (144 other events, 10016.1 us)
Sparse Core Ops, SparseCore 0:
  91.9 41.3 all-gather.8
  135.1 22.4 all-gather.6
Sparse Core Ops, SparseCore 1:
  100.4 26.8 reduce-scatter.11
  1897.6 18.8 reduce-scatter.9
  1918.5 16.1 reduce-scatter.13
  2050.1 65.9 all-reduce.4
